TPU v7x, 32 devices: a 4x4x1 block of a 4x4x8 slice. The times are simulated.
32 devices in a mesh: spin: 1 (over z), depth: 4 (over y), row: 4 (over x), col: 2 (over core).
Axes of the slice: x: 4, y: 4, z: 1, core: 2. Of those that a mesh axis runs over, the one named last changes fastest.
The devices are a block of a 4x4x8 slice.
Arguments:
- hamiltonian: float32 [2, 3584, 3584], P('spin', 'row', 'col')
- spec_bounds: float32 [2, 2], P('spin')
- occ_count: int32 [2], P('spin')
Outputs:
- output 1: float32 [2, 3584, 3584], P('spin', 'row', 'col')
- output 2: float32 [2], P('spin')
All inputs are finite; a program needn't handle non-finite values.
Results may differ from a plain program's by a relative error of at most 0.001.
Values sent between devices are 32-bit elements.
A program may use at most 768 MiB of HBM per device.

v0:
```python
import jax
import jax.numpy as jnp
from jax import lax
from jax.sharding import PartitionSpec as P

STEPS = 3


def solution(mesh):
    depth_size = mesh.shape['depth']
    row_size = mesh.shape['row']
    col_size = mesh.shape['col']
    per_col = row_size // col_size
    highest = lax.Precision.HIGHEST

    def local_purify(ham_blk, spec_bounds, occ_count):
        kpoints, row_blk, col_blk = ham_blk.shape
        mat_order = col_blk * col_size
        sub_width = row_blk // depth_size
        row_idx = lax.axis_index('row')
        col_idx = lax.axis_index('col')
        layer_idx = lax.axis_index('depth')
        on_diag = (row_idx // per_col) == col_idx
        diag_start = (row_idx % per_col) * row_blk

        def diag_trace(mat_blk):
            square = lax.dynamic_slice_in_dim(mat_blk, diag_start, row_blk, axis=2)
            return jnp.where(on_diag, jnp.trace(square, axis1=1, axis2=2), 0.0)

        def left_operand(mat_blk):
            pieces = mat_blk.reshape(kpoints, row_blk, per_col, depth_size, sub_width)
            own_piece = lax.dynamic_index_in_dim(pieces, layer_idx, axis=3, keepdims=False)
            own_piece = own_piece.reshape(kpoints, row_blk, per_col * sub_width)
            return lax.all_gather(own_piece, 'col', axis=2, tiled=True)

        def right_operand(mat_blk):
            pieces = mat_blk.reshape(kpoints, depth_size, sub_width, col_blk)
            own_piece = lax.dynamic_index_in_dim(pieces, layer_idx, axis=1, keepdims=False)
            return lax.all_gather(own_piece, 'row', axis=1, tiled=True)

        def product(left_op, right_op):
            partial_prod = jnp.einsum('kab,kbc->kac', left_op, right_op, precision=highest, preferred_element_type=jnp.float32)
            return lax.psum(partial_prod, 'depth')

        occupied = occ_count.astype(jnp.float32)
        chem_pot = lax.psum(diag_trace(ham_blk), ('row', 'col')) / mat_order
        scale_fac = jnp.minimum(occupied / (spec_bounds[:, 1] - chem_pot), (mat_order - occupied) / (chem_pot - spec_bounds[:, 0]))
        diag_add = (scale_fac * chem_pot + occupied) / mat_order
        row_ids = lax.broadcasted_iota(jnp.int32, (row_blk, col_blk), 0) + row_idx * row_blk
        col_ids = lax.broadcasted_iota(jnp.int32, (row_blk, col_blk), 1) + col_idx * col_blk
        eye_blk = (row_ids == col_ids).astype(jnp.float32)
        density = diag_add[:, None, None] * eye_blk - (scale_fac / mat_order)[:, None, None] * ham_blk
        for step_idx in range(STEPS):
            dens_right = right_operand(density)
            dens_sq = product(left_operand(density), dens_right)
            dens_cube = product(left_operand(dens_sq), dens_right)
            local_traces = jnp.stack([diag_trace(density), jnp.sum(density * density, axis=(1, 2)), jnp.sum(dens_sq * density, axis=(1, 2))])
            traces = lax.psum(local_traces, ('row', 'col'))
            purify_coef = ((traces[1] - traces[2]) / (traces[0] - traces[1]))[:, None, None]
            density = ((1.0 - 2.0 * purify_coef) * density + (1.0 + purify_coef) * dens_sq - dens_cube) / (1.0 - purify_coef)
        energy = 2.0 * lax.psum(jnp.sum(density * ham_blk, axis=(1, 2)), ('row', 'col'))
        return density, energy

    mat_spec = P('spin', 'row', 'col')
    return jax.shard_map(local_purify, mesh=mesh, in_specs=(mat_spec, P('spin', None), P('spin')), out_specs=(mat_spec, P('spin')), check_vma=False)
```

profile of v0, /device:TPU:97, one launch (start us, length us, event | category | flops | bytes accessed | tf_op | source)
XLA Modules:
  0.0 2401.2 jit_solution(7366600925196666295)
XLA Ops:
  7.3 0.2 iota_compare_fusion
  7.5 1.0 slice_reduce_fusion.1
  8.5 3.8 select_reduce_fusion.3
  12.4 13.8 psum.77
  26.2 0.7 add_multiply_fusion
  26.9 0.5 compare_convert_fusion
  27.4 2.7 copy-done
  30.1 10.6 multiply_subtract_fusion
  40.7 13.2 copy.13
  53.9 3.8 constant_dynamic-slice_fusion.5
  57.8 0.1 all-gather.25.cloned.1.call-start
  57.8 3.8 dynamic-slice_bitcast_fusion.2
  61.7 0.1 all-reduce.7.cloned.1.call-start
  61.8 16.6 all-gather.13.cloned.1.call-done
  78.4 121.2 %all-gather.25.cloned.1.call-done = f32[2,1,896,1792]{3,2,0,1:T(8,128)} async-done(((f32[2,1,224,1792]{3,2,0,1:T(8,128)}), f32[2,1,896,1792]{3,2,0,1:T(8,128)}) %all-gather.25.cloned.1.call-update) | async-done | bytes 12845072 | tf_op jit(solution)/shard_map/all_gather | solution.py:39
  199.6 48.2 %fusion.10 = f32[2,896,1792]{2,1,0:T(8,128)} fusion(f32[2,896,896]{1,2,0:T(8,128)} %all-gather.13.cloned.1.call-done, f32[2,1,896,1792]{3,2,0,1:T(8,128)} %all-gather.25.cloned.1.call-done), kind=kOutput, calls=%fused_computation.10 | convolution fusion | flops 34527510528 | bytes 32112640 | tf_op jit(solution)/shard_map/kab,kbc->kac/dot_general | solution.py:42
  247.9 228.0 %all-reduce.7.cloned.1.call-done = f32[2,896,1792]{2,1,0:T(8,128)} async-done(((f32[2,896,1792]{2,1,0:T(8,128)}), f32[2,896,1792]{2,1,0:T(8,128)}) %all-reduce.7.cloned.1.call-update) | async-done | bytes 12845072 | tf_op jit(solution)/shard_map/psum | solution.py:43
  475.9 13.2 copy.15
  489.1 3.8 constant_dynamic-slice_fusion.4
  493.1 18.2 all-gather.15.cloned.1.call-done
  511.3 63.0 %fusion.8 = f32[2,896,1792]{2,1,0:T(8,128)} fusion(f32[2,896,896]{1,2,0:T(8,128)} %all-gather.15.cloned.1.call-done, f32[2,1,896,1792]{3,2,0,1:T(8,128)} %all-gather.25.cloned.1.call-done), kind=kOutput, calls=%fused_computation.8 | convolution fusion | flops 34527510528 | bytes 32112640 | tf_op jit(solution)/shard_map/kab,kbc->kac/dot_general | solution.py:42
  574.4 3.8 select_reduce_fusion.2
  578.2 12.3 multiply_reduce_fusion.6
  590.5 12.6 psum.79
  603.2 199.1 %all-reduce.9.cloned.1.call-done = f32[2,896,1792]{2,1,0:T(8,128)} async-done(((f32[2,896,1792]{2,1,0:T(8,128)}), f32[2,896,1792]{2,1,0:T(8,128)}) %all-reduce.9.cloned.1.call-update) | async-done | bytes 12845072 | tf_op jit(solution)/shard_map/psum | solution.py:43
  802.2 20.1 subtract_divide_fusion.2
  822.4 13.2 copy.16
  835.6 3.9 constant_dynamic-slice_fusion.3
  839.5 0.1 all-gather.27.cloned.1.call-start
  839.6 3.8 dynamic-slice_bitcast_fusion.1
  843.6 14.2 all-gather.17.cloned.1.call-done
  857.8 121.2 %all-gather.27.cloned.1.call-done = f32[2,1,896,1792]{3,2,0,1:T(8,128)} async-done(((f32[2,1,224,1792]{3,2,0,1:T(8,128)}), f32[2,1,896,1792]{3,2,0,1:T(8,128)}) %all-gather.27.cloned.1.call-update) | async-done | bytes 12845072 | tf_op jit(solution)/shard_map/all_gather | solution.py:39
  979.0 48.3 %fusion.6 = f32[2,896,1792]{2,1,0:T(8,128)} fusion(f32[2,896,896]{1,2,0:T(8,128)} %all-gather.17.cloned.1.call-done, f32[2,1,896,1792]{3,2,0,1:T(8,128)} %all-gather.27.cloned.1.call-done), kind=kOutput, calls=%fused_computation.6 | convolution fusion | flops 34527510528 | bytes 32112640 | tf_op jit(solution)/shard_map/kab,kbc->kac/dot_general | solution.py:42
  1027.4 0.1 all-gather.19.cloned.1.call-start
  1027.4 228.0 %all-reduce.11.cloned.1.call-done = f32[2,896,1792]{2,1,0:T(8,128)} async-done(((f32[2,896,1792]{2,1,0:T(8,128)}), f32[2,896,1792]{2,1,0:T(8,128)}) %all-reduce.11.cloned.1.call-update) | async-done | bytes 12845072 | tf_op jit(solution)/shard_map/psum | solution.py:43
  1255.4 13.2 copy.18
  1268.6 3.8 constant_dynamic-slice_fusion.2
  1272.5 18.2 all-gather.19.cloned.1.call-done
  1290.7 63.1 %fusion.4 = f32[2,896,1792]{2,1,0:T(8,128)} fusion(f32[2,896,896]{1,2,0:T(8,128)} %all-gather.19.cloned.1.call-done, f32[2,1,896,1792]{3,2,0,1:T(8,128)} %all-gather.27.cloned.1.call-done), kind=kOutput, calls=%fused_computation.4 | convolution fusion | flops 34527510528 | bytes 32112640 | tf_op jit(solution)/shard_map/kab,kbc->kac/dot_general | solution.py:42
  1353.9 3.8 select_reduce_fusion.1
  1357.8 9.4 multiply_reduce_fusion.4
  1367.2 12.6 psum.82
  1379.8 202.0 %all-reduce.13.cloned.1.call-done = f32[2,896,1792]{2,1,0:T(8,128)} async-done(((f32[2,896,1792]{2,1,0:T(8,128)}), f32[2,896,1792]{2,1,0:T(8,128)}) %all-reduce.13.cloned.1.call-update) | async-done | bytes 12845072 | tf_op jit(solution)/shard_map/psum | solution.py:43
  1581.8 18.1 subtract_divide_fusion.1
  1599.9 13.2 copy.19
  1613.1 3.9 constant_dynamic-slice_fusion.1
  1617.1 0.1 all-gather.29.cloned.1.call-start
  1617.1 3.8 dynamic-slice_bitcast_fusion
  1621.1 14.2 all-gather.21.cloned.1.call-done
  1635.3 121.1 %all-gather.29.cloned.1.call-done = f32[2,1,896,1792]{3,2,0,1:T(8,128)} async-done(((f32[2,1,224,1792]{3,2,0,1:T(8,128)}), f32[2,1,896,1792]{3,2,0,1:T(8,128)}) %all-gather.29.cloned.1.call-update) | async-done | bytes 12845072 | tf_op jit(solution)/shard_map/all_gather | solution.py:39
  1756.5 48.3 %fusion.2 = f32[2,896,1792]{2,1,0:T(8,128)} fusion(f32[2,896,896]{1,2,0:T(8,128)} %all-gather.21.cloned.1.call-done, f32[2,1,896,1792]{3,2,0,1:T(8,128)} %all-gather.29.cloned.1.call-done), kind=kOutput, calls=%fused_computation.2 | convolution fusion | flops 34527510528 | bytes 32112640 | tf_op jit(solution)/shard_map/kab,kbc->kac/dot_general | solution.py:42
  1804.8 0.1 all-gather.23.cloned.1.call-start
  1804.9 228.0 %all-reduce.15.cloned.1.call-done = f32[2,896,1792]{2,1,0:T(8,128)} async-done(((f32[2,896,1792]{2,1,0:T(8,128)}), f32[2,896,1792]{2,1,0:T(8,128)}) %all-reduce.15.cloned.1.call-update) | async-done | bytes 12845072 | tf_op jit(solution)/shard_map/psum | solution.py:43
  2032.8 13.2 copy.21
  2046.0 3.8 constant_dynamic-slice_fusion
  2049.9 18.2 all-gather.23.cloned.1.call-done
  2068.2 62.9 %fusion = f32[2,896,1792]{2,1,0:T(8,128)} fusion(f32[2,896,896]{1,2,0:T(8,128)} %all-gather.23.cloned.1.call-done, f32[2,1,896,1792]{3,2,0,1:T(8,128)} %all-gather.29.cloned.1.call-done), kind=kOutput, calls=%fused_computation | convolution fusion | flops 34527510528 | bytes 32112640 | tf_op jit(solution)/shard_map/kab,kbc->kac/dot_general | solution.py:42
  2131.1 3.8 select_reduce_fusion
  2134.9 9.4 multiply_reduce_fusion.2
  2144.3 12.6 psum.85
  2157.0 202.0 %all-reduce.17.cloned.1.call-done = f32[2,896,1792]{2,1,0:T(8,128)} async-done(((f32[2,896,1792]{2,1,0:T(8,128)}), f32[2,896,1792]{2,1,0:T(8,128)}) %all-reduce.17.cloned.1.call-update) | async-done | bytes 12845072 | tf_op jit(solution)/shard_map/psum | solution.py:43
  2359.0 22.1 multiply_reduce_fusion
  2381.2 12.7 psum.87
  2393.9 0.5 broadcast_multiply_fusion
  (41 shorter events, 1.5 us)
Async XLA Ops:
  7.2 71.2 %all-gather.13.cloned.1.call-start = ((), (), s32[]{:S(2)}) async-start(), calls=%async_computation | async-start | bytes 9633792 | tf_op jit(solution)/shard_map/all_gather | solution.py:34
  27.4 2.7 copy-start
  57.8 141.8 %all-gather.25.cloned.1.call-start = ((), (), s32[]{:S(2)}) async-start(), calls=%async_computation.12 | async-start | bytes 16056320 | tf_op jit(solution)/shard_map/all_gather | solution.py:39
  61.7 414.2 %all-reduce.7.cloned.1.call-start = ((), (), s32[]{:S(2)}) async-start(), calls=%async_computation.1 | async-start | bytes 25690112 | tf_op jit(solution)/shard_map/psum | solution.py:43
  247.9 263.4 %all-gather.15.cloned.1.call-start = ((), (), s32[]{:S(2)}) async-start(), calls=%async_computation.2 | async-start | bytes 9633792 | tf_op jit(solution)/shard_map/all_gather | solution.py:34
  493.0 309.3 %all-reduce.9.cloned.1.call-start = ((), (), s32[]{:S(2)}) async-start(), calls=%async_computation.3 | async-start | bytes 25690112 | tf_op jit(solution)/shard_map/psum | solution.py:43
  574.3 283.5 %all-gather.17.cloned.1.call-start = ((), (), s32[]{:S(2)}) async-start(), calls=%async_computation.4 | async-start | bytes 9633792 | tf_op jit(solution)/shard_map/all_gather | solution.py:34
  839.5 139.5 %all-gather.27.cloned.1.call-start = ((), (), s32[]{:S(2)}) async-start(), calls=%async_computation.13 | async-start | bytes 16056320 | tf_op jit(solution)/shard_map/all_gather | solution.py:39
  843.5 411.9 %all-reduce.11.cloned.1.call-start = ((), (), s32[]{:S(2)}) async-start(), calls=%async_computation.5 | async-start | bytes 25690112 | tf_op jit(solution)/shard_map/psum | solution.py:43
  1027.4 263.4 %all-gather.19.cloned.1.call-start = ((), (), s32[]{:S(2)}) async-start(), calls=%async_computation.6 | async-start | bytes 9633792 | tf_op jit(solution)/shard_map/all_gather | solution.py:34
  1272.5 309.4 %all-reduce.13.cloned.1.call-start = ((), (), s32[]{:S(2)}) async-start(), calls=%async_computation.7 | async-start | bytes 25690112 | tf_op jit(solution)/shard_map/psum | solution.py:43
  1353.9 281.5 %all-gather.21.cloned.1.call-start = ((), (), s32[]{:S(2)}) async-start(), calls=%async_computation.8 | async-start | bytes 9633792 | tf_op jit(solution)/shard_map/all_gather | solution.py:34
  1617.1 139.4 %all-gather.29.cloned.1.call-start = ((), (), s32[]{:S(2)}) async-start(), calls=%async_computation.14 | async-start | bytes 16056320 | tf_op jit(solution)/shard_map/all_gather | solution.py:39
  1621.1 411.8 %all-reduce.15.cloned.1.call-start = ((), (), s32[]{:S(2)}) async-start(), calls=%async_computation.9 | async-start | bytes 25690112 | tf_op jit(solution)/shard_map/psum | solution.py:43
  1804.8 263.4 %all-gather.23.cloned.1.call-start = ((), (), s32[]{:S(2)}) async-start(), calls=%async_computation.10 | async-start | bytes 9633792 | tf_op jit(solution)/shard_map/all_gather | solution.py:34
  2049.9 309.2 %all-reduce.17.cloned.1.call-start = ((), (), s32[]{:S(2)}) async-start(), calls=%async_computation.11 | async-start | bytes 25690112 | tf_op jit(solution)/shard_map/psum | solution.py:43
Sparse Core Ops, SparseCore 0:
  57.9 20.4 all-gather.12
  79.9 119.6 all-gather.24
  248.0 227.8 all-reduce.6
  493.1 18.1 all-gather.14
  574.4 227.7 all-reduce.8
  839.6 18.1 all-gather.16
  859.4 119.6 all-gather.26
  1027.5 227.8 all-reduce.10
  1272.6 18.1 all-gather.18
  1354.0 227.7 all-reduce.12
  1617.2 18.1 all-gather.20
  1636.8 119.6 all-gather.28
  1804.9 227.8 all-reduce.14
  2050.0 18.1 all-gather.22
  2131.2 227.7 all-reduce.16
where the time goes:
time: 2410 us; the launch traced here: 2400 us
  waiting for transfers between devices  1750 us (73%)
  matrix products  334 us (14%)
  other arithmetic  119 us (5%)
  local copies, waits for them, and re-layouts  117 us (5%)
  blocking collectives  64.5 us (3%)
    psum x6, waiting for transfers between devices, product(): return lax.psum(partial_prod, 'depth')  1290 us
    all_gather x3, waiting for transfers between devices, right_operand(): return lax.all_gather(own_piece, 'row', axis=1, tiled=True)  364 us
    dot_general x6, matrix products, product(): jnp.einsum('kab,kbc->kac', left_op, right_op, precision=highest, preferre...  334 us
    all_gather x6, waiting for transfers between devices, left_operand(): return lax.all_gather(own_piece, 'col', axis=2, tiled=True)  99.7 us
  transfers between devices with their start and end apart: 15, of which 15 were waited for; matrix products, arithmetic and copies ran while one was open for 2% of the time, Pallas kernels for 0%

commit v1 on v0

v1 whole, which is shorter than its diff:
```python
import functools

import jax
import jax.numpy as jnp
from jax import lax
from jax.experimental import pallas as pl
from jax.experimental.pallas import tpu as pltpu
from jax.sharding import PartitionSpec as P

STEPS = 3
MESH = pl.DeviceIdType.MESH
LANE = 128
HIGHEST = lax.Precision.HIGHEST


class Geometry:
    def __init__(self, mesh, ham_shape):
        kpoints, self.blk, self.half = ham_shape
        self.depth = mesh.shape["depth"]
        self.rows = mesh.shape["row"]
        self.cols = mesh.shape["col"]
        self.kpoints = kpoints
        self.layers = self.depth // kpoints
        self.order = self.half * self.cols
        self.strip = self.blk // (self.layers * self.cols)
        self.lo = self.blk // 2 // LANE * LANE
        self.wide = self.blk - self.lo
        assert self.rows == 4 and self.cols == 2 and self.layers == 2 and self.depth == 4


def rem(a, b):
    return lax.rem(a, b)


def gather_kernel(geo, strip_ref, full_ref, send_sem, recv_sem, sib_send, sib_recv, local_sem):
    d = lax.axis_index("depth")
    r = lax.axis_index("row")
    c = lax.axis_index("col")
    e = rem(d, geo.layers)
    mate = d + 1 - 2 * e
    up, down = rem(r + 1, 4), rem(r + 3, 4)
    to_up, to_down, to_mate = {"row": up}, {"row": down}, {"depth": mate}
    to_sib = {"col": 1 - c}

    barrier = pltpu.get_barrier_semaphore()
    for dev in (to_up, to_down, to_mate, to_sib):
        pl.semaphore_signal(barrier, inc=1, device_id=dev, device_id_type=MESH)
    pl.semaphore_wait(barrier, 4)

    hh = geo.strip // 2

    def place(lam, delta, h, part, core):
        rr = rem(r + delta, 4)
        ee = e if lam == 0 else 1 - e
        row0 = rr * geo.blk + (ee * 2 + core) * geo.strip
        size = geo.strip
        if h is not None:
            row0, size = row0 + h * hh, hh
        if part < 2:
            col0, width = rem(rr + part, 4) * geo.blk, geo.blk
        else:
            col0 = rem(rr + 2, 4) * geo.blk + geo.lo * rem(rr // 2 + ee, 2)
            width = geo.wide
        return (pl.ds(pl.multiple_of(row0, 8), size), pl.ds(pl.multiple_of(col0, LANE), width))

    slots = {(lam, delta, h): i for i, (lam, delta, h) in enumerate(
        [(lam, delta, h) for lam in (0, 1) for delta, h in ((0, None), (1, None), (3, None), (2, 0), (2, 1))])}

    def branch(core):
        started = []

        def send(src, there, dev, part, n):
            here = place(*src, part, core)
            if src == (0, 0, None):
                rows, cols = here
                ref = strip_ref.at[:, cols]
            else:
                ref = full_ref.at[here]
            cp = pltpu.make_async_remote_copy(
                src_ref=ref, dst_ref=full_ref.at[here],
                send_sem=send_sem.at[n, part], recv_sem=recv_sem.at[slots[there], part],
                device_id=dev, device_id_type=MESH)
            cp.start()
            started.append(cp)

        def sib(slot, part):
            here = place(*slot, part, core)
            ref = strip_ref.at[:, here[1]] if slot == (0, 0, None) else full_ref.at[here]
            cp = pltpu.make_async_remote_copy(
                src_ref=ref, dst_ref=full_ref.at[here],
                send_sem=sib_send.at[slots[slot], part], recv_sem=sib_recv.at[slots[slot], part],
                device_id=to_sib, device_id_type=MESH)
            cp.start()
            started.append(cp)

        def half(slot, h):
            return (slot[0], slot[1], h)

        def arrive(slot, part):
            here = place(*slot, part, core)
            pltpu.make_async_copy(full_ref.at[here], full_ref.at[here], recv_sem.at[slots[slot], part]).wait()

        def send_half(src, h, there, dev, part, n):
            rr_src = (src[0], src[1], h)
            here = place(*rr_src, part, core)
            cp = pltpu.make_async_remote_copy(
                src_ref=full_ref.at[here], dst_ref=full_ref.at[here],
                send_sem=send_sem.at[n, part], recv_sem=recv_sem.at[slots[there], part],
                device_id=dev, device_id_type=MESH)
            cp.start()
            started.append(cp)

        own, mate_own = (0, 0, None), (1, 0, None)
        below = lambda lam: (lam, 3, None)
        above = lambda lam: (lam, 1, None)
        far = lambda lam, h: (lam, 2, h)
        for p in range(3):
            send(own, mate_own, to_mate, p, 0)
            send(own, below(0), to_up, p, 1)
            send(own, above(0), to_down, p, 2)
        for p in range(3):
            sib(own, p)
        if core == 0:
            for p in range(3):
                arrive(mate_own, p)
                send(mate_own, below(1), to_up, p, 3)
                send(mate_own, above(1), to_down, p, 4)
                sib(mate_own, p)
            for lam in (0, 1):
                for p in range(3):
                    arrive(below(lam), p)
                    send_half(below(lam), 0, far(lam, 0), to_up, p, 5 + 2 * lam)
                    sib(below(lam), p)
                    arrive(above(lam), p)
                    send_half(above(lam), 1, far(lam, 1), to_down, p, 6 + 2 * lam)
                    sib(above(lam), p)
            for lam in (0, 1):
                for p in range(3):
                    for h in (0, 1):
                        arrive(far(lam, h), p)
                        sib(far(lam, h), p)
        else:
            for p in range(3):
                arrive(below(0), p)
                send_half(below(0), 0, far(0, 0), to_up, p, 3)
                send(below(0), below(1), to_mate, p, 4)
                sib(below(0), p)
                arrive(above(0), p)
                send_half(above(0), 1, far(0, 1), to_down, p, 5)
                send(above(0), above(1), to_mate, p, 6)
                sib(above(0), p)
            for p in range(3):
                arrive(mate_own, p)
                sib(mate_own, p)
            for p in range(3):
                for h in (0, 1):
                    arrive(far(0, h), p)
                    send(far(0, h), far(1, h), to_mate, p, 7 + h)
                    sib(far(0, h), p)
            for p in range(3):
                for slot in (below(1), above(1)):
                    arrive(slot, p)
                    sib(slot, p)
            for p in range(3):
                for h in (0, 1):
                    arrive(far(1, h), p)
                    sib(far(1, h), p)
        for slot in slots:
            for p in range(3):
                here = place(*slot, p, 1 - core)
                pltpu.make_async_copy(full_ref.at[here], full_ref.at[here], sib_recv.at[slots[slot], p]).wait()
        for cp in started:
            cp.wait_send()

    row0 = r * geo.blk + (e * 2 + c) * geo.strip
    keep = pltpu.make_async_copy(strip_ref, full_ref.at[pl.ds(pl.multiple_of(row0, 8), geo.strip)], local_sem)
    keep.start()
    pl.when(c == 0)(lambda: branch(0))
    pl.when(c == 1)(lambda: branch(1))
    keep.wait()


def gather(geo, strip, call):
    return pl.pallas_call(
        functools.partial(gather_kernel, geo),
        out_shape=jax.ShapeDtypeStruct((geo.order, geo.order), jnp.float32),
        in_specs=[pl.BlockSpec(memory_space=pltpu.VMEM)],
        out_specs=pl.BlockSpec(memory_space=pl.ANY),
        scratch_shapes=[
            pltpu.SemaphoreType.DMA((9, 3)),
            pltpu.SemaphoreType.DMA((10, 3)),
            pltpu.SemaphoreType.DMA((10, 3)),
            pltpu.SemaphoreType.DMA((10, 3)),
            pltpu.SemaphoreType.DMA,
        ],
        compiler_params=pltpu.CompilerParams(collective_id=call, has_side_effects=True),
        name="gather",
    )(strip)


def mirror(geo, full):
    blk, lo, wide = geo.blk, geo.lo, geo.wide
    per = blk // LANE
    shape = jax.ShapeDtypeStruct(full.shape, full.dtype)

    def body(src_ref, dst_ref):
        dst_ref[...] = src_ref[...].T

    full = pl.pallas_call(
        body, grid=(4, per), out_shape=shape,
        in_specs=[pl.BlockSpec((LANE, blk), lambda i, t: (i * per + t, (i + 1) % 4))],
        out_specs=pl.BlockSpec((blk, LANE), lambda i, t: ((i + 1) % 4, i * per + t)),
        input_output_aliases={0: 0}, name="mirror_next",
    )(full)

    def rows_of(i, t):
        return pl.multiple_of(i * blk + t * wide, LANE)

    def cols_of(i, t):
        return pl.multiple_of((i + 2) % 4 * blk + lo * ((i // 2 + t) % 2), LANE)

    return pl.pallas_call(
        body, grid=(4, 2), out_shape=shape,
        in_specs=[pl.BlockSpec((pl.Element(lo), pl.Element(wide)), lambda i, t: (rows_of(i, t), cols_of(i, t)))],
        out_specs=pl.BlockSpec((pl.Element(wide), pl.Element(lo)), lambda i, t: (cols_of(i, t), rows_of(i, t))),
        input_output_aliases={0: 0}, name="mirror_far",
    )(full)


def spread_kernel(geo, strip_ref, out_ref, send_sem, recv_sem, sib_send, sib_recv, local_sem):
    d = lax.axis_index("depth")
    c = lax.axis_index("col")
    up, down = {"depth": rem(d + 1, 4)}, {"depth": rem(d + 3, 4)}
    to_sib = {"col": 1 - c}
    barrier = pltpu.get_barrier_semaphore()
    for dev in (up, down, to_sib):
        pl.semaphore_signal(barrier, inc=1, device_id=dev, device_id_type=MESH)
    pl.semaphore_wait(barrier, 3)

    hh = geo.strip // 2

    def place(delta, core, h):
        dd = rem(d + delta, 4)
        row0 = (rem(dd, geo.layers) * 2 + core) * geo.strip
        size = geo.strip
        if h is not None:
            row0, size = row0 + h * hh, hh
        return (dd // geo.layers, pl.ds(pl.multiple_of(row0, 8), size))

    slots = {(0, None): 0, (1, None): 1, (3, None): 2, (2, 0): 3, (2, 1): 4}
    mine = pl.ds(pl.multiple_of(c * geo.half, LANE), geo.half)
    other = pl.ds(pl.multiple_of((1 - c) * geo.half, LANE), geo.half)
    started = []

    def send(src, dst, there, who, dev, n):
        cp = pltpu.make_async_remote_copy(
            src_ref=src, dst_ref=dst, send_sem=send_sem.at[n, who], recv_sem=recv_sem.at[slots[there], who],
            device_id=dev, device_id_type=MESH)
        cp.start()
        started.append(cp)

    cp = pltpu.make_async_remote_copy(
        src_ref=strip_ref.at[:, other], dst_ref=out_ref.at[place(0, c, None)], send_sem=sib_send, recv_sem=sib_recv,
        device_id=to_sib, device_id_type=MESH)
    cp.start()
    started.append(cp)
    keep = pltpu.make_async_copy(strip_ref.at[:, mine], out_ref.at[place(0, c, None)], local_sem)
    keep.start()
    own = out_ref.at[place(0, c, None)]
    send(strip_ref.at[:, mine], own, (3, None), 0, up, 0)
    send(strip_ref.at[:, mine], own, (1, None), 0, down, 1)
    sibs = out_ref.at[place(0, 1 - c, None)]
    pltpu.make_async_copy(sibs, sibs, sib_recv).wait()
    send(sibs, sibs, (3, None), 1, up, 0)
    send(sibs, sibs, (1, None), 1, down, 1)

    def arrive(delta, h, who):
        ref = out_ref.at[place(delta, c if who == 0 else 1 - c, h)]
        pltpu.make_async_copy(ref, ref, recv_sem.at[slots[(delta, h)], who]).wait()

    for who in (0, 1):
        core = c if who == 0 else 1 - c
        arrive(3, None, who)
        ref = out_ref.at[place(3, core, 0)]
        send(ref, ref, (2, 0), who, up, 2)
        arrive(1, None, who)
        ref = out_ref.at[place(1, core, 1)]
        send(ref, ref, (2, 1), who, down, 3)
    for who in (0, 1):
        arrive(2, 0, who)
        arrive(2, 1, who)
    keep.wait()
    for cp in started:
        cp.wait_send()


def spread(geo, strip, call):
    return pl.pallas_call(
        functools.partial(spread_kernel, geo),
        out_shape=jax.ShapeDtypeStruct((geo.kpoints, geo.blk, geo.half), jnp.float32),
        in_specs=[pl.BlockSpec(memory_space=pltpu.VMEM)],
        out_specs=pl.BlockSpec(memory_space=pl.ANY),
        scratch_shapes=[
            pltpu.SemaphoreType.DMA((4, 2)),
            pltpu.SemaphoreType.DMA((5, 2)),
            pltpu.SemaphoreType.DMA,
            pltpu.SemaphoreType.DMA,
            pltpu.SemaphoreType.DMA,
        ],
        compiler_params=pltpu.CompilerParams(collective_id=call, has_side_effects=True),
        name="spread",
    )(strip)


def solution(mesh):
    def local_purify(ham, spec_bounds, occ_count):
        geo = Geometry(mesh, ham.shape)
        n = geo.order
        d = lax.axis_index("depth")
        r = lax.axis_index("row")
        c = lax.axis_index("col")
        m, e = d // geo.layers, d % geo.layers
        per_col = geo.rows // geo.cols
        on_diag = (r // per_col) == c
        diag_start = (r % per_col) * geo.blk
        square = lax.dynamic_slice_in_dim(ham, diag_start, geo.blk, axis=2)
        tr = jnp.where(on_diag, jnp.trace(square, axis1=1, axis2=2), 0.0)
        mu = lax.psum(tr, ("row", "col")) / n
        occ = occ_count.astype(jnp.float32)
        lam = jnp.minimum(occ / (spec_bounds[:, 1] - mu), (n - occ) / (mu - spec_bounds[:, 0]))
        add = (lam * mu + occ) / n
        scale = lam / n

        row0 = r * geo.blk + (e * 2 + c) * geo.strip
        rows = lax.broadcasted_iota(jnp.int32, (geo.strip, n), 0) + row0
        cols = lax.broadcasted_iota(jnp.int32, (geo.strip, n), 1)
        diag = rows == cols

        ham_m = lax.dynamic_index_in_dim(ham, m, axis=0, keepdims=False)
        layer_rows = lax.dynamic_slice_in_dim(ham_m, e * 2 * geo.strip, 2 * geo.strip, axis=0)
        layer_all = lax.all_gather(layer_rows, "col", axis=1, tiled=True)
        ham_strip = lax.dynamic_slice_in_dim(layer_all, c * geo.strip, geo.strip, axis=0)
        strip = jnp.where(diag, add[m], 0.0) - scale[m] * ham_strip

        for step in range(STEPS):
            full = mirror(geo, gather(geo, strip, step))
            sq = jnp.dot(strip, full, precision=HIGHEST, preferred_element_type=jnp.float32)
            sums = jnp.stack([jnp.sum(jnp.where(diag, strip, 0.0)), jnp.sum(strip * strip), jnp.sum(sq * strip)])
            slot = (jnp.arange(geo.kpoints) == m).astype(jnp.float32)
            traces = lax.psum(slot[:, None] * sums[None, :], ("depth", "row", "col"))
            t = lax.dynamic_index_in_dim(traces, m, axis=0, keepdims=False)
            coef = (t[1] - t[2]) / (t[0] - t[1])
            cube = jnp.dot(sq, full, precision=HIGHEST, preferred_element_type=jnp.float32)
            strip = ((1.0 - 2.0 * coef) * strip + (1.0 + coef) * sq - cube) / (1.0 - coef)
        density = spread(geo, strip, STEPS)
        energy = 2.0 * lax.psum(jnp.sum(density * ham, axis=(1, 2)), ("row", "col"))
        return density, energy

    mat = P("spin", "row", "col")
    return jax.shard_map(
        local_purify, mesh=mesh, in_specs=(mat, P("spin", None), P("spin")), out_specs=(mat, P("spin")), check_vma=False)
```

time: 2410 us -> 1060 us (0.44)
  waiting for transfers between devices: 1750 us -> 2.73 us
  Pallas kernels: 0 us -> 554 us
  local copies, waits for them, and re-layouts: 117 us -> 17.3 us
  blocking collectives: 64.5 us -> 161 us
  other arithmetic: 119 us -> 25.1 us
  matrix products: 334 us -> 267 us
    psum x6 -> x0, waiting for transfers between devices: 1290 us -> none  [product(): return lax.psum(partial_prod, 'depth')]
    pallas_call x0 -> x10, Pallas kernels: none -> 554 us  [the longest x3 354 us: gather(): pl.pallas_call(functools.partial(gather_kernel, geo), out_shape=jax.Shape...]
    all_gather x9 -> x1, waiting for transfers between devices: 463 us -> 2.68 us  [local_purify(): layer_all = lax.all_gather(layer_rows, 'col', axis=1, tiled=True)]
    psum x5, blocking collectives: 64.5 us -> 161 us  [the longest x3 134 us: local_purify(): traces = lax.psum(slot[:, None] * sums[None, :], ('depth', 'row', 'col'))]
    dot_general x6, matrix products: 334 us -> 267 us  [the longest x3 134 us: local_purify(): jnp.dot(sq, full, precision=HIGHEST, preferred_element_type=jnp.float32)]
    reduce_sum x8 -> x2, other arithmetic: 68.6 us -> 13.2 us  [the longest x1 9.32 us: local_purify(): energy = 2.0 * lax.psum(jnp.sum(density * ham, axis=(1, 2)), ('row', 'col'))]
    psum x3 -> x0, local copies, waits for them, and re-layouts: 39.6 us -> none  [product(): return lax.psum(partial_prod, 'depth')]
    div x4 -> x2, other arithmetic: 38.9 us -> 0.02 us  [the longest x1 0.01 us: local_purify(): add = (lam * mu + occ) / n]
  transfers between devices with their start and end apart: 15 -> 1, of which waited for: 15 -> 1; matrix products, arithmetic and copies ran while one was open for 2% -> 1% of each run, Pallas kernels for 0% -> 0%
where the time goes in v1:
time: 1060 us; the launch traced here: 1050 us
  Pallas kernels  554 us (52%)
  matrix products  267 us (25%)
  blocking collectives  161 us (15%)
  other arithmetic  25.1 us (2%)
  between operations  21.8 us (2%)
  local copies, waits for them, and re-layouts  17.3 us (2%)
    pallas_call x3, Pallas kernels, gather(): pl.pallas_call(functools.partial(gather_kernel, geo), out_shape=jax.Shape...  354 us
    psum x3, blocking collectives, local_purify(): traces = lax.psum(slot[:, None] * sums[None, :], ('depth', 'row', 'col'))  134 us
    dot_general x3, matrix products, local_purify(): jnp.dot(sq, full, precision=HIGHEST, preferred_element_type=jnp.float32)  134 us
    dot_general x3, matrix products, local_purify(): jnp.dot(strip, full, precision=HIGHEST, preferred_element_type=jnp.float32)  133 us
    pallas_call x1, Pallas kernels, spread(): pl.pallas_call(functools.partial(spread_kernel, geo), out_shape=jax.Shape...  108 us
    pallas_call x3, Pallas kernels, mirror(): pl.pallas_call(body, grid=(4, per), out_shape=shape, in_specs=[pl.BlockSp...  64.3 us
    pallas_call x3, Pallas kernels, mirror(): pl.pallas_call(body, grid=(4, 2), out_shape=shape, in_specs=[pl.BlockSpec...  26.6 us
  transfers between devices with their start and end apart: 1, of which 1 were waited for; matrix products, arithmetic and copies ran while one was open for 1% of the time, Pallas kernels for 0%

profile of v1, /device:TPU:97, one launch (start us, length us, event | category | flops | bytes accessed | tf_op | source)
XLA Modules:
  0.0 1049.1 jit_solution(805810985918910519)
XLA Ops:
  7.2 0.1 all-gather.3.cloned.1.call-start
  7.3 3.9 constant_dynamic-slice_fusion.3
  11.2 0.1 all-gather.3.cloned.1.call-update
  11.2 0.2 iota_compare_fusion
  11.5 0.0 copy-start.3
  11.5 0.0 copy-start.4
  11.5 3.9 select_reduce_fusion
  15.4 13.8 %psum.35 = f32[2]{0:T(128)S(1)} all-reduce(f32[2]{0:T(128)S(1)} %broadcast_select_fusion), channel_id=1, replica_groups=mesh['spin'=1,'depth'=4,'row'=4,'col'=2] {'row','col'}, use_global_device_ids=true, to_apply=%region_1.2 | all-reduce | flops 2 | bytes 16 | tf_op jit(solution)/shard_map/psum | solution.py:328
  29.2 0.0 copy-done.3
  29.2 0.2 slice_reduce_fusion.1
  29.4 0.0 copy-done.4
  29.4 0.6 dynamic_slice.30
  30.0 0.6 dynamic_slice.31
  30.6 2.7 all-gather.3.cloned.1.call-done
  33.3 5.3 bitcast_subtract_fusion.strip_ref
  38.6 119.6 %gather.3.src_ref = f32[3584,3584]{1,0:T(8,128)} custom-call(f32[224,3584]{1,0:T(8,128)} %bitcast_subtract_fusion.strip_ref), custom_call_target="tpu_custom_call" | custom-call | tf_op jit(solution)/shard_map/gather/pallas_call | solution.py:184
  158.2 21.4 %mirror_next.3.src_ref = f32[3584,3584]{1,0:T(8,128)} custom-call(f32[3584,3584]{1,0:T(8,128)} %gather.3.src_ref), custom_call_target="tpu_custom_call", output_to_operand_aliasing={{}: (0, {})} | custom-call | tf_op jit(solution)/shard_map/mirror_next/pallas_call | solution.py:209
  179.6 0.0 copy-start
  179.6 8.9 mirror_far.3
  188.5 0.0 copy-done
  188.5 44.5 %select_reduce_fusion.3 = (f32[]{:T(128)}, f32[]{:T(128)}, f32[]{:T(128)}, f32[224,3584]{1,0:T(8,128)}) fusion(f32[224,3584]{1,0:T(8,128)S(1)} %copy-done, s32[224]{0:T(256)S(1)} %iota_add_fusion, f32[3584,3584]{1,0:T(8,128)} %mirror_far.3), kind=kOutput, calls=%fused_computation.17 | convolution fusion | flops 34533130240 | bytes 57803660 | tf_op jit(solution)/shard_map/dot_general | solution.py:347
  233.0 1.9 pad_maximum_fusion
  234.8 0.1 broadcast_multiply_fusion.2
  234.9 44.7 %psum.36 = f32[2,3]{1,0:T(2,128)S(1)} all-reduce(f32[2,3]{1,0:T(2,128)S(1)} %broadcast_multiply_fusion.2), channel_id=1, replica_groups=mesh['spin'=1,'depth'=4,'row'=4,'col'=2] {'depth','row','col'}, use_global_device_ids=true, to_apply=%region_5.6 | all-reduce | flops 6 | bytes 48 | tf_op jit(solution)/shard_map/psum | solution.py:350
  279.7 0.6 fusion.5
  282.6 44.7 %fusion.strip_ref = f32[224,3584]{1,0:T(8,128)} fusion(f32[224,3584]{1,0:T(8,128)} %get-tuple-element.24, f32[3584,3584]{1,0:T(8,128)} %mirror_far.3, f32[224,3584]{1,0:T(8,128)S(1)} %copy-done, f32[]{:T(128)} %bitcast.8, f32[]{:T(128)} %bitcast.7, f32[]{:T(128)} %bitcast.6), kind=kOutput, calls=%fused_computation.5 | convolution fusion | flops 34531524608 | bytes 61014028 | tf_op jit(solution)/shard_map/dot_general | solution.py:353
  327.3 117.5 %gather.4.src_ref = f32[3584,3584]{1,0:T(8,128)} custom-call(f32[224,3584]{1,0:T(8,128)} %fusion.strip_ref), custom_call_target="tpu_custom_call" | custom-call | tf_op jit(solution)/shard_map/gather/pallas_call | solution.py:184
  444.8 21.4 %mirror_next.4.src_ref = f32[3584,3584]{1,0:T(8,128)} custom-call(f32[3584,3584]{1,0:T(8,128)} %gather.4.src_ref), custom_call_target="tpu_custom_call", output_to_operand_aliasing={{}: (0, {})} | custom-call | tf_op jit(solution)/shard_map/mirror_next/pallas_call | solution.py:209
  466.2 0.0 copy-start.2
  466.2 8.9 mirror_far.4
  475.1 0.0 copy-done.2
  475.1 44.5 %select_reduce_fusion.2 = (f32[]{:T(128)}, f32[]{:T(128)}, f32[]{:T(128)}, f32[224,3584]{1,0:T(8,128)}) fusion(f32[224,3584]{1,0:T(8,128)S(1)} %copy-done.2, s32[224]{0:T(256)S(1)} %iota_add_fusion, f32[3584,3584]{1,0:T(8,128)} %mirror_far.4), kind=kOutput, calls=%fused_computation.14 | convolution fusion | flops 34533130240 | bytes 57803660 | tf_op jit(solution)/shard_map/dot_general | solution.py:347
  519.6 1.9 pad_maximum_fusion.1
  521.4 0.1 broadcast_multiply_fusion.1
  521.5 44.7 %psum.37 = f32[2,3]{1,0:T(2,128)S(1)} all-reduce(f32[2,3]{1,0:T(2,128)S(1)} %broadcast_multiply_fusion.1), channel_id=1, replica_groups=mesh['spin'=1,'depth'=4,'row'=4,'col'=2] {'depth','row','col'}, use_global_device_ids=true, to_apply=%region_9.10 | all-reduce | flops 6 | bytes 48 | tf_op jit(solution)/shard_map/psum | solution.py:350
  566.2 0.6 fusion.4
  569.2 44.7 %fusion.1.strip_ref = f32[224,3584]{1,0:T(8,128)} fusion(f32[224,3584]{1,0:T(8,128)} %get-tuple-element.25, f32[3584,3584]{1,0:T(8,128)} %mirror_far.4, f32[224,3584]{1,0:T(8,128)S(1)} %copy-done.2, f32[]{:T(128)} %bitcast.14, f32[]{:T(128)} %bitcast.13, f32[]{:T(128)} %bitcast.12), kind=kOutput, calls=%fused_computation.6 | convolution fusion | flops 34531524608 | bytes 61014028 | tf_op jit(solution)/shard_map/dot_general | solution.py:353
  613.8 117.3 %gather.5.src_ref = f32[3584,3584]{1,0:T(8,128)} custom-call(f32[224,3584]{1,0:T(8,128)} %fusion.1.strip_ref), custom_call_target="tpu_custom_call" | custom-call | tf_op jit(solution)/shard_map/gather/pallas_call | solution.py:184
  731.1 21.4 %mirror_next.5.src_ref = f32[3584,3584]{1,0:T(8,128)} custom-call(f32[3584,3584]{1,0:T(8,128)} %gather.5.src_ref), custom_call_target="tpu_custom_call", output_to_operand_aliasing={{}: (0, {})} | custom-call | tf_op jit(solution)/shard_map/mirror_next/pallas_call | solution.py:209
  752.6 0.0 copy-start.1
  752.6 8.9 mirror_far.5
  761.4 0.0 copy-done.1
  761.4 44.5 %select_reduce_fusion.1 = (f32[]{:T(128)}, f32[]{:T(128)}, f32[]{:T(128)}, f32[224,3584]{1,0:T(8,128)}) fusion(f32[224,3584]{1,0:T(8,128)S(1)} %copy-done.1, s32[224]{0:T(256)S(1)} %iota_add_fusion, f32[3584,3584]{1,0:T(8,128)} %mirror_far.5), kind=kOutput, calls=%fused_computation.11 | convolution fusion | flops 34533130240 | bytes 57803660 | tf_op jit(solution)/shard_map/dot_general | solution.py:347
  805.9 1.9 pad_maximum_fusion.2
  807.8 0.1 broadcast_multiply_fusion
  807.8 44.7 %psum.38 = f32[2,3]{1,0:T(2,128)S(1)} all-reduce(f32[2,3]{1,0:T(2,128)S(1)} %broadcast_multiply_fusion), channel_id=1, replica_groups=mesh['spin'=1,'depth'=4,'row'=4,'col'=2] {'depth','row','col'}, use_global_device_ids=true, to_apply=%region_13.14 | all-reduce | flops 6 | bytes 48 | tf_op jit(solution)/shard_map/psum | solution.py:350
  852.6 0.6 fusion.3
  855.6 44.7 %fusion.2.strip_ref = f32[224,3584]{1,0:T(8,128)} fusion(f32[224,3584]{1,0:T(8,128)} %get-tuple-element.26, f32[3584,3584]{1,0:T(8,128)} %mirror_far.5, f32[224,3584]{1,0:T(8,128)S(1)} %copy-done.1, f32[]{:T(128)} %bitcast.20, f32[]{:T(128)} %bitcast.19, f32[]{:T(128)} %bitcast.18), kind=kOutput, calls=%fused_computation.7 | convolution fusion | flops 34531524608 | bytes 61014028 | tf_op jit(solution)/shard_map/dot_general | solution.py:353
  900.2 108.2 %spread.1 = f32[2,896,1792]{2,1,0:T(8,128)} custom-call(f32[224,3584]{1,0:T(8,128)} %fusion.2.strip_ref), custom_call_target="tpu_custom_call" | custom-call | tf_op jit(solution)/shard_map/spread/pallas_call | solution.py:298
  1008.5 9.3 multiply_reduce_fusion
  1017.8 13.2 %psum.39 = f32[2]{0:T(128)S(1)} all-reduce(f32[2]{0:T(128)S(1)} %multiply_reduce_fusion), channel_id=1, replica_groups=mesh['spin'=1,'depth'=4,'row'=4,'col'=2] {'row','col'}, use_global_device_ids=true, to_apply=%region_15.16 | all-reduce | flops 2 | bytes 16 | tf_op jit(solution)/shard_map/psum | solution.py:356
  1031.0 0.5 broadcast_multiply_fusion.3
  1031.5 10.3 copy.18
  (8 shorter events, 0.0 us)
Async XLA Ops:
  7.2 26.1 %all-gather.3.cloned.1.call-start = ((), (), s32[]{:S(2)}) async-start(), calls=%async_computation | async-start | bytes 9633792 | tf_op jit(solution)/shard_map/all_gather | solution.py:341
  11.5 17.7 %copy-start.3 = (f32[2,2]{1,0:T(2,128)S(1)}, f32[2,2]{1,0:T(2,128)}, u32[]{:S(2)}) copy-start(f32[2,2]{1,0:T(2,128)} %param.4) | copy-start | bytes 52
  11.5 17.9 %copy-start.4 = (s32[2]{0:T(128)S(1)}, s32[2]{0:T(128)}, u32[]{:S(2)}) copy-start(s32[2]{0:T(128)} %param.5) | copy-start | bytes 28
  179.6 8.9 copy-start
  466.2 8.9 copy-start.2
  752.6 8.9 copy-start.1
Sparse Core Ops, SparseCore 0:
  11.3 21.8 all-gather.2

commit v2 on v0

v2 whole, which is shorter than its diff:
```python
import functools

import jax
import jax.numpy as jnp
from jax import lax
from jax.experimental import pallas as pl
from jax.experimental.pallas import tpu as pltpu
from jax.sharding import PartitionSpec as P

STEPS = 3
MESH = pl.DeviceIdType.MESH
LANE = 128
HIGHEST = lax.Precision.HIGHEST


class Geometry:
    def __init__(self, mesh, ham_shape):
        kpoints, self.blk, self.half = ham_shape
        self.depth = mesh.shape["depth"]
        self.rows = mesh.shape["row"]
        self.cols = mesh.shape["col"]
        self.kpoints = kpoints
        self.layers = self.depth // kpoints
        self.order = self.half * self.cols
        self.strip = self.blk // (self.layers * self.cols)
        self.lo = self.blk // 2 // LANE * LANE
        self.wide = self.blk - self.lo
        self.chunk = 4 * LANE
        self.chunks = self.order // self.chunk
        assert self.rows == 4 and self.cols == 2 and self.layers == 2 and self.depth == 4


def rem(a, b):
    return lax.rem(a, b)


class Links:
    def __init__(self, geo, own_ref, full_ref, send_sem, recv_sem, sib_send, sib_recv):
        self.geo, self.own, self.full = geo, own_ref, full_ref
        self.send_sem, self.recv_sem, self.sib_send, self.sib_recv = send_sem, recv_sem, sib_send, sib_recv
        d = lax.axis_index("depth")
        self.r = lax.axis_index("row")
        self.c = lax.axis_index("col")
        self.e = rem(d, geo.layers)
        self.up, self.down = {"row": rem(self.r + 1, 4)}, {"row": rem(self.r + 3, 4)}
        self.mate = {"depth": d + 1 - 2 * self.e}
        self.sibling = {"col": 1 - self.c}
        self.drained = set()
        self.slots = {slot: i for i, slot in enumerate(
            [(lam, delta, h) for lam in (0, 1) for delta, h in ((0, None), (1, None), (3, None), (2, 0), (2, 1))])}

    def place(self, slot, part, core):
        geo = self.geo
        lam, delta, h = slot
        rr = rem(self.r + delta, 4)
        ee = self.e if lam == 0 else 1 - self.e
        row0 = rr * geo.blk + (ee * 2 + core) * geo.strip
        size = geo.strip
        if h is not None:
            row0, size = row0 + h * (geo.strip // 2), geo.strip // 2
        if part < 2:
            col0, width = rem(rr + part, 4) * geo.blk, geo.blk
        else:
            col0 = rem(rr + 2, 4) * geo.blk + geo.lo * rem(rr // 2 + ee, 2)
            width = geo.wide
        return pl.ds(pl.multiple_of(row0, 8), size), pl.ds(pl.multiple_of(col0, LANE), width)

    def copy(self, src, there, dev, part, core, n):
        here = self.place(src, part, core)
        ref = self.own.at[:, here[1]] if src == OWN else self.full.at[here]
        return pltpu.make_async_remote_copy(
            src_ref=ref, dst_ref=self.full.at[here], send_sem=self.send_sem.at[n, part],
            recv_sem=self.recv_sem.at[self.slots[there], part], device_id=dev, device_id_type=MESH)

    def sib_copy(self, slot, part, core):
        here = self.place(slot, part, core)
        ref = self.own.at[:, here[1]] if slot == OWN else self.full.at[here]
        i = self.slots[slot]
        return pltpu.make_async_remote_copy(
            src_ref=ref, dst_ref=self.full.at[here], send_sem=self.sib_send.at[i, part],
            recv_sem=self.sib_recv.at[i, part], device_id=self.sibling, device_id_type=MESH)

    def arrive(self, slot, part, core):
        here = self.full.at[self.place(slot, part, core)]
        pltpu.make_async_copy(here, here, self.recv_sem.at[self.slots[slot], part]).wait()

    def sib_arrive(self, slot, part, core):
        here = self.full.at[self.place(slot, part, 1 - core)]
        pltpu.make_async_copy(here, here, self.sib_recv.at[self.slots[slot], part]).wait()

    def sends(self, core):
        table = [(OWN, MATE, self.mate), (OWN, below(0), self.up), (OWN, above(0), self.down)]
        lams = (0, 1) if core == 0 else (0,)
        if core == 0:
            table += [(MATE, below(1), self.up), (MATE, above(1), self.down)]
        for lam in lams:
            table += [((lam, 3, 0), far(lam, 0), self.up), ((lam, 1, 1), far(lam, 1), self.down)]
        if core == 1:
            table += [(below(0), below(1), self.mate), (above(0), above(1), self.mate)]
            table += [(far(0, h), far(1, h), self.mate) for h in (0, 1)]
        return table

    def forward(self, slot, part, core):
        for n, (src, there, dev) in enumerate(self.sends(core)):
            if src == slot or (slot[2] is None and slot[1] in (1, 3) and src[:2] == slot[:2] and src[2] is not None):
                self.copy(src, there, dev, part, core, n).start()
        self.sib_copy(slot, part, core).start()

    def relay(self, slot, part, core):
        self.arrive(slot, part, core)
        self.forward(slot, part, core)

    def drain(self, slots, parts, core):
        for part in parts:
            for n, (src, there, dev) in enumerate(self.sends(core)):
                whole = src[:2] + ((None,) if src[1] != 2 else (src[2],))
                if whole in slots and (core, n, part) not in self.drained:
                    self.drained.add((core, n, part))
                    self.copy(src, there, dev, part, core, n).wait_send()
            for slot in slots:
                if (core, slot, part) not in self.drained:
                    self.drained.add((core, slot, part))
                    self.sib_copy(slot, part, core).wait_send()


OWN, MATE = (0, 0, None), (1, 0, None)


def below(lam):
    return (lam, 3, None)


def above(lam):
    return (lam, 1, None)


def far(lam, h):
    return (lam, 2, h)


def per_core(c, fn):
    pl.when(c == 0)(lambda: fn(0))
    pl.when(c == 1)(lambda: fn(1))


class Reduce:
    def __init__(self, geo, src, mid, box, send, recv):
        self.src, self.mid, self.box, self.send, self.recv = src, mid, box, send, recv
        d, r, c = (lax.axis_index(a) for a in ("depth", "row", "col"))
        mate = d + 1 - 2 * rem(d, geo.layers)
        self.round1 = [{"row": rem(r + k, 4)} for k in (1, 2, 3)]
        self.round2 = [{"depth": mate}, {"col": 1 - c}, {"depth": mate, "col": 1 - c}]

    def copies(self, first):
        devs, src, base = (self.round1, self.src, 0) if first else (self.round2, self.mid, 3)
        return [pltpu.make_async_remote_copy(
            src_ref=src, dst_ref=self.box.at[base + i], send_sem=self.send.at[base + i], recv_sem=self.recv.at[base + i],
            device_id=dev, device_id_type=MESH) for i, dev in enumerate(devs)]

    def start(self, first):
        for cp in self.copies(first):
            cp.start()

    def total(self, first):
        for cp in self.copies(first):
            cp.wait()
        base = 0 if first else 3
        src = self.src if first else self.mid
        return (src[...] + self.box[base]) + (self.box[base + 1] + self.box[base + 2])


def enter(devs):
    barrier = pltpu.get_barrier_semaphore()
    for dev in devs:
        pl.semaphore_signal(barrier, inc=1, device_id=dev, device_id_type=MESH)
    pl.semaphore_wait(barrier, len(devs))


def transpose_region(full, row0, col0, h, w, tin, tout, sem):
    rows, cols = pl.ds(pl.multiple_of(row0, LANE), h), pl.ds(pl.multiple_of(col0, LANE), w)
    cp = pltpu.make_async_copy(full.at[rows, cols], tin.at[pl.ds(0, h), pl.ds(0, w)], sem)
    cp.start()
    cp.wait()

    def body(t, carry):
        at = pl.ds(pl.multiple_of(t * LANE, LANE), LANE)
        tout[pl.ds(0, w), at] = tin[at, pl.ds(0, w)].T
        return carry

    lax.fori_loop(0, h // LANE, body, 0)
    out = full.at[pl.ds(pl.multiple_of(col0, LANE), w), pl.ds(pl.multiple_of(row0, LANE), h)]
    cp = pltpu.make_async_copy(tout.at[pl.ds(0, w), pl.ds(0, h)], out, sem)
    cp.start()
    cp.wait()


def mirror_next(geo, full, k, tin, tout, sem):
    k = rem(k, 4)
    transpose_region(full, k * geo.blk, rem(k + 1, 4) * geo.blk, geo.blk, geo.blk, tin, tout, sem)


def mirror_far(geo, full, k, tin, tout, sem):
    def body(j, carry):
        i, t = rem(k + 2 * (j // 2), 4), rem(j, 2)
        row0 = i * geo.blk + t * geo.wide
        col0 = rem(i + 2, 4) * geo.blk + geo.lo * rem(i // 2 + t, 2)
        transpose_region(full, row0, col0, geo.lo, geo.wide, tin, tout, sem)
        return carry

    lax.fori_loop(0, 4, body, 0)


def complete(geo, links, core, keeps, tin, tout, sem, done):
    full, r = links.full, links.r
    near = (MATE,) if core == 0 else (below(0), above(0))
    for part in range(done, 3):
        for slot in near:
            links.relay(slot, part, core)
    if core == 0:
        for lam in (0, 1):
            for part in range(3):
                links.relay(below(lam), part, core)
                links.relay(above(lam), part, core)
    else:
        for part in range(3):
            links.relay(MATE, part, core)
        for part in range(3):
            for h in (0, 1):
                links.relay(far(0, h), part, core)
    for cp in keeps:
        cp.wait()

    def sibs(slots):
        for slot in slots:
            for part in range(3):
                links.sib_arrive(slot, part, core)

    sibs((OWN, MATE))
    mirror_next(geo, full, r, tin, tout, sem)
    if core == 1:
        for part in range(3):
            links.relay(below(1), part, core)
            links.relay(above(1), part, core)
    sibs((below(0), below(1), above(0), above(1)))
    mirror_next(geo, full, r + 3, tin, tout, sem)
    mirror_next(geo, full, r + 1, tin, tout, sem)
    links.drain((below(0), below(1), above(0), above(1)), (2,), core)
    mirror_far(geo, full, r + 1, tin, tout, sem)
    for part in range(3):
        for lam in (0, 1) if core == 0 else (1,):
            for h in (0, 1):
                links.relay(far(lam, h), part, core)
    sibs([far(lam, h) for lam in (0, 1) for h in (0, 1)])
    mirror_next(geo, full, r + 2, tin, tout, sem)
    links.drain([slot for slot in links.slots if slot[1] in (0, 2)], (2,), core)
    mirror_far(geo, full, r, tin, tout, sem)
    links.drain(list(links.slots), range(3), core)


def keep_copy(links, own, part, sem):
    geo = links.geo
    row0 = links.r * geo.blk + (links.e * 2 + links.c) * geo.strip
    cols = pl.ds(pl.multiple_of(rem(links.r + part, 4) * geo.blk, LANE), geo.blk)
    return pltpu.make_async_copy(own.at[:, cols], links.full.at[pl.ds(pl.multiple_of(row0, 8), geo.strip), cols], sem.at[part])


def first_kernel(geo, strip, full, send_sem, recv_sem, sib_send, sib_recv, keep_sem, tin, tout, tsem):
    links = Links(geo, strip, full, send_sem, recv_sem, sib_send, sib_recv)
    enter([links.up, links.down, links.mate, links.sibling])
    keeps = [keep_copy(links, strip, part, keep_sem) for part in range(4)]

    def run(core):
        for part in range(3):
            links.forward(OWN, part, core)
        for cp in keeps:
            cp.start()
        complete(geo, links, core, keeps, tin, tout, tsem, 0)

    per_core(links.c, run)


def cube_loop(geo, red, first_block, full_in, sq, strip, new, buf, acc, buf_sem, hook):
    per, size, blk = geo.chunks, geo.chunk, geo.blk

    def cols_of(part):
        return pl.ds(pl.multiple_of(rem(first_block + part, 4) * blk, LANE), blk)

    def load(i):
        rows = pl.ds(pl.multiple_of(rem(i, per) * size, LANE), size)
        slot = rem(i, 2)
        return pltpu.make_async_copy(full_in.at[rows, cols_of(i // per)], buf.at[slot], buf_sem.at[slot])

    load(0).start()

    def body(i, carry):
        k = rem(i, per)

        @pl.when(i + 1 < 4 * per)
        def _():
            load(i + 1).start()

        load(i).wait()

        @pl.when(k == 0)
        def _():
            acc[...] = jnp.zeros_like(acc)

        acc[...] += jnp.dot(sq[:, pl.ds(pl.multiple_of(k * size, LANE), size)], buf[rem(i, 2)],
                            precision=HIGHEST, preferred_element_type=jnp.float32)

        @pl.when(i == 1)
        def _():
            red.mid[...] = red.total(True)

        @pl.when(i == 3)
        def _():
            red.start(False)

        @pl.when(i == per - 1)
        def _():
            red.src_total[...] = red.total(False)

        @pl.when(k == per - 1)
        def _():
            cols = cols_of(i // per)
            t1, t2, t3 = (red.src_total[j:j + 1, 0:1] for j in range(3))
            coef = (t2 - t3) / (t1 - t2)
            new[:, cols] = ((1.0 - 2.0 * coef) * strip[:, cols] + (1.0 + coef) * sq[:, cols] - acc[...]) / (1.0 - coef)

        hook(i)
        return carry

    lax.fori_loop(0, 4 * per, body, 0)


def mid_kernel(geo, full_in, sq, strip, sums, full, new, send_sem, recv_sem, sib_send, sib_recv, keep_sem, tin, tout, tsem,
               buf, acc, buf_sem, mid, tot, box, red_send, red_recv):
    links = Links(geo, new, full, send_sem, recv_sem, sib_send, sib_recv)
    red = Reduce(geo, sums, mid, box, red_send, red_recv)
    red.src_total = tot
    enter(red.round1 + red.round2)
    red.start(True)
    keeps = [keep_copy(links, new, part, keep_sem) for part in range(4)]

    def hook(i):
        for part in range(3):
            @pl.when(i == (part + 1) * geo.chunks)
            def _():
                per_core(links.c, lambda core: links.forward(OWN, part, core))
                keeps[part].start()

        @pl.when(i == 3 * geo.chunks)
        def _():
            def early(core):
                for slot in (MATE,) if core == 0 else (below(0), above(0)):
                    links.relay(slot, 0, core)
            per_core(links.c, early)

    cube_loop(geo, red, links.r, full_in, sq, strip, new, buf, acc, buf_sem, hook)
    keeps[3].start()
    per_core(links.c, lambda core: complete(geo, links, core, keeps, tin, tout, tsem, 1))


def last_kernel(geo, full_in, sq, strip, sums, ham, dens, energy, new, send_sem, recv_sem, sib_send, sib_recv, keep_sem,
                buf, acc, buf_sem, mid, tot, box, red_send, red_recv, esum, emid, ebox, eother, esend, erecv):
    d, r, c = (lax.axis_index(a) for a in ("depth", "row", "col"))
    blk, strip_rows, layers = geo.blk, geo.strip, geo.layers
    red = Reduce(geo, sums, mid, box, red_send, red_recv)
    red.src_total = tot
    ered = Reduce(geo, esum, emid, ebox, esend, erecv)
    up, down, across = ({"depth": rem(d + k, 4)} for k in (1, 3, 2))
    sibling = {"col": 1 - c}
    enter(red.round1 + [up, down, across, sibling, red.round2[2]])
    red.start(True)
    hh = strip_rows // 2
    slots = {(0, None): 0, (1, None): 1, (3, None): 2, (2, 0): 3, (2, 1): 4}

    def place(delta, who, h, q):
        core = c if who == 0 else 1 - c
        dd = rem(d + delta, 4)
        row0, size = (rem(dd, layers) * 2 + core) * strip_rows, strip_rows
        if h is not None:
            row0, size = row0 + h * hh, hh
        return dens.at[dd // layers, pl.ds(pl.multiple_of(row0, 8), size), pl.ds(q * blk, blk)]

    def cols_of(part):
        return pl.ds(pl.multiple_of(rem(2 * c + part, 4) * blk, LANE), blk)

    def copy(src, dst, there, who, q, dev, n):
        return pltpu.make_async_remote_copy(
            src_ref=src, dst_ref=dst, send_sem=send_sem.at[n, who, q], recv_sem=recv_sem.at[slots[there], who, q],
            device_id=dev, device_id_type=MESH)

    def out_copies(who, q):
        here = place(0, who, None, q)
        src = new.at[:, cols_of(q)] if who == 0 else here
        return [copy(src, here, (3, None), who, q, up, 0), copy(src, here, (1, None), who, q, down, 1)]

    def half_copies(who, q):
        top, low = place(3, who, 0, q), place(1, who, 1, q)
        return [copy(top, top, (2, 0), who, q, up, 2), copy(low, low, (2, 1), who, q, down, 3)]

    def sib_copy(q):
        return pltpu.make_async_remote_copy(
            src_ref=new.at[:, cols_of(2 + q)], dst_ref=place(0, 0, None, q), send_sem=sib_send.at[q],
            recv_sem=sib_recv.at[q], device_id=sibling, device_id_type=MESH)

    def arrive(delta, h, who, q):
        ref = place(delta, who, h, q)
        pltpu.make_async_copy(ref, ref, recv_sem.at[slots[(delta, h)], who, q]).wait()

    keeps = [pltpu.make_async_copy(new.at[:, cols_of(q)], place(0, 0, None, q), keep_sem.at[q]) for q in (0, 1)]

    def relay(who, q):
        halves = half_copies(who, q)
        arrive(3, None, who, q)
        halves[0].start()
        arrive(1, None, who, q)
        halves[1].start()

    def energy_part(part):
        cols = cols_of(part)
        s = jnp.sum(new[:, cols] * ham[:, cols], axis=0, keepdims=True)
        s = jnp.sum(s, axis=1, keepdims=True)
        part_sum = jnp.broadcast_to(s, esum.shape)
        esum[...] = part_sum if part == 0 else esum[...] + part_sum

    def hook(i):
        for part in range(4):
            if part < 3:
                at = i == (part + 1) * geo.chunks

                @pl.when(at)
                def _():
                    if part < 2:
                        for cp in out_copies(0, part):
                            cp.start()
                        keeps[part].start()
                    else:
                        sib_copy(part - 2).start()

            @pl.when(i == (part + 1) * geo.chunks - 1)
            def _():
                energy_part(part)

    cube_loop(geo, red, 2 * c, full_in, sq, strip, new, buf, acc, buf_sem, hook)

    def sibling_out(q):
        ref = place(0, 1, None, q)
        pltpu.make_async_copy(ref, ref, sib_recv.at[q]).wait()
        for cp in out_copies(1, q):
            cp.start()

    sibling_out(0)
    sib_copy(1).start()
    ered.start(True)
    sibling_out(1)
    emid_val = ered.total(True)
    emid[...] = emid_val
    for q in (0, 1):
        relay(0, q)
    ered.start(False)
    for q in (0, 1):
        relay(1, q)
    tot[...] = ered.total(False)
    for who in (0, 1):
        for q in (0, 1):
            for h in (0, 1):
                arrive(2, h, who, q)
    swap = pltpu.make_async_remote_copy(
        src_ref=tot, dst_ref=eother, send_sem=esend.at[6], recv_sem=erecv.at[6], device_id=across, device_id_type=MESH)
    swap.start()
    for cp in keeps:
        cp.wait()
    for who in (0, 1):
        for q in (0, 1):
            for cp in out_copies(who, q) + half_copies(who, q):
                cp.wait_send()
    for q in (0, 1):
        sib_copy(q).wait_send()
    swap.wait()
    mine_first = (d // layers) == 0
    row = lax.broadcasted_iota(jnp.int32, energy.shape, 0)
    a, b = tot[...], eother[...]
    low = jnp.where(mine_first, a, b)
    high = jnp.where(mine_first, b, a)
    energy[...] = 2.0 * jnp.where(row == 0, low, high)


VM = pl.BlockSpec(memory_space=pltpu.VMEM)
ANY = pl.BlockSpec(memory_space=pl.ANY)
DMA = pltpu.SemaphoreType.DMA
TILE = (8, LANE)


def link_scratch(geo):
    return [DMA((9, 3)), DMA((10, 3)), DMA((10, 3)), DMA((10, 3)), DMA((4,)),
            pltpu.VMEM((geo.blk, geo.blk), jnp.float32), pltpu.VMEM((geo.blk, geo.blk), jnp.float32), DMA]


def cube_scratch(geo):
    return [pltpu.VMEM((2, geo.chunk, geo.blk), jnp.float32), pltpu.VMEM((geo.strip, geo.blk), jnp.float32), DMA((2,)),
            pltpu.VMEM(TILE, jnp.float32), pltpu.VMEM(TILE, jnp.float32), pltpu.VMEM((6, *TILE), jnp.float32),
            DMA((6,)), DMA((6,))]


def params(call):
    return pltpu.CompilerParams(collective_id=call, has_side_effects=True)


def first(geo, strip, call):
    return pl.pallas_call(
        functools.partial(first_kernel, geo), name="first",
        out_shape=jax.ShapeDtypeStruct((geo.order, geo.order), jnp.float32),
        in_specs=[VM], out_specs=ANY, scratch_shapes=link_scratch(geo), compiler_params=params(call))(strip)


def middle(geo, full, sq, strip, sums, call):
    return pl.pallas_call(
        functools.partial(mid_kernel, geo), name="middle",
        out_shape=(jax.ShapeDtypeStruct((geo.order, geo.order), jnp.float32),
                   jax.ShapeDtypeStruct((geo.strip, geo.order), jnp.float32)),
        in_specs=[ANY, VM, VM, VM], out_specs=(ANY, VM), scratch_shapes=link_scratch(geo) + cube_scratch(geo),
        compiler_params=params(call))(full, sq, strip, sums)


def last(geo, full, sq, strip, sums, ham, call):
    one = pltpu.VMEM(TILE, jnp.float32)
    return pl.pallas_call(
        functools.partial(last_kernel, geo), name="last",
        out_shape=(jax.ShapeDtypeStruct((geo.kpoints, geo.blk, geo.half), jnp.float32),
                   jax.ShapeDtypeStruct(TILE, jnp.float32)),
        in_specs=[ANY, VM, VM, VM, VM], out_specs=(ANY, VM),
        scratch_shapes=[pltpu.VMEM((geo.strip, geo.order), jnp.float32), DMA((4, 2, 2)), DMA((5, 2, 2)), DMA((2,)), DMA((2,)),
                        DMA((2,))] + cube_scratch(geo) + [one, one, pltpu.VMEM((6, *TILE), jnp.float32), one, DMA((7,)), DMA((7,))],
        compiler_params=params(call))(full, sq, strip, sums, ham)


def solution(mesh):
    def local_purify(ham, spec_bounds, occ_count):
        geo = Geometry(mesh, ham.shape)
        n = geo.order
        d = lax.axis_index("depth")
        r = lax.axis_index("row")
        c = lax.axis_index("col")
        m, e = d // geo.layers, d % geo.layers
        per_col = geo.rows // geo.cols
        on_diag = (r // per_col) == c
        diag_start = (r % per_col) * geo.blk
        square = lax.dynamic_slice_in_dim(ham, diag_start, geo.blk, axis=2)
        tr = jnp.where(on_diag, jnp.trace(square, axis1=1, axis2=2), 0.0)
        mu = lax.psum(tr, ("row", "col")) / n
        occ = occ_count.astype(jnp.float32)
        lam = jnp.minimum(occ / (spec_bounds[:, 1] - mu), (n - occ) / (mu - spec_bounds[:, 0]))
        add = (lam * mu + occ) / n
        scale = lam / n

        row0 = r * geo.blk + (e * 2 + c) * geo.strip
        rows = lax.broadcasted_iota(jnp.int32, (geo.strip, n), 0) + row0
        cols = lax.broadcasted_iota(jnp.int32, (geo.strip, n), 1)
        diag = rows == cols

        ham_m = lax.dynamic_index_in_dim(ham, m, axis=0, keepdims=False)
        layer_rows = lax.dynamic_slice_in_dim(ham_m, e * 2 * geo.strip, 2 * geo.strip, axis=0)
        layer_all = lax.all_gather(layer_rows, "col", axis=1, tiled=True)
        ham_strip = lax.dynamic_slice_in_dim(layer_all, c * geo.strip, geo.strip, axis=0)
        strip = jnp.where(diag, add[m], 0.0) - scale[m] * ham_strip

        full = first(geo, strip, 0)
        for step in range(STEPS):
            sq = jnp.dot(strip, full, precision=HIGHEST, preferred_element_type=jnp.float32)
            sums = jnp.stack([jnp.sum(jnp.where(diag, strip, 0.0)), jnp.sum(strip * strip), jnp.sum(sq * strip)])
            sums = jnp.broadcast_to(jnp.pad(sums, (0, 5))[:, None], TILE)
            if step < STEPS - 1:
                full, strip = middle(geo, full, sq, strip, sums, step + 1)
        density, pair = last(geo, full, sq, strip, sums, ham_strip, STEPS)
        energy = pair[:geo.kpoints, 0]
        return density, energy

    mat = P("spin", "row", "col")
    return jax.shard_map(
        local_purify, mesh=mesh, in_specs=(mat, P("spin", None), P("spin")), out_specs=(mat, P("spin")), check_vma=False)
```

time: 2410 us -> 797 us (0.33)
  waiting for transfers between devices: 1750 us -> 2.74 us
  Pallas kernels: 0 us -> 587 us
  matrix products: 334 us -> 136 us
  other arithmetic: 119 us -> 16.4 us
  local copies, waits for them, and re-layouts: 117 us -> 18.9 us
  blocking collectives: 64.5 us -> 13.8 us
    psum x6 -> x0, waiting for transfers between devices: 1290 us -> none  [product(): return lax.psum(partial_prod, 'depth')]
    pallas_call x0 -> x4, Pallas kernels: none -> 587 us  [the longest x2 314 us: middle(): pl.pallas_call(functools.partial(mid_kernel, geo), name='middle', out_sha...]
    all_gather x9 -> x1, waiting for transfers between devices: 463 us -> 2.68 us  [local_purify(): layer_all = lax.all_gather(layer_rows, 'col', axis=1, tiled=True)]
    dot_general x6 -> x3, matrix products: 334 us -> 136 us  [local_purify(): jnp.dot(strip, full, precision=HIGHEST, preferred_element_type=jnp.float32)]
    reduce_sum x8 -> x1, other arithmetic: 68.6 us -> 3.86 us  [local_purify(): tr = jnp.where(on_diag, jnp.trace(square, axis1=1, axis2=2), 0.0)]
    psum x5 -> x1, blocking collectives: 64.5 us -> 13.8 us  [local_purify(): mu = lax.psum(tr, ('row', 'col')) / n]
    psum x3 -> x0, local copies, waits for them, and re-layouts: 39.6 us -> none  [product(): return lax.psum(partial_prod, 'depth')]
    div x4 -> x2, other arithmetic: 38.9 us -> 0.02 us  [the longest x1 0.01 us: local_purify(): add = (lam * mu + occ) / n]
  transfers between devices with their start and end apart: 15 -> 1, of which waited for: 15 -> 1; matrix products, arithmetic and copies ran while one was open for 2% -> 1% of each run, Pallas kernels for 0% -> 0%
where the time goes in v2:
time: 797 us; the launch traced here: 790 us
  Pallas kernels  587 us (74%)
  matrix products  136 us (17%)
  local copies, waits for them, and re-layouts  18.9 us (2%)
  other arithmetic  16.4 us (2%)
  between operations  14.6 us (2%)
  blocking collectives  13.8 us (2%)
    pallas_call x2, Pallas kernels, middle(): pl.pallas_call(functools.partial(mid_kernel, geo), name='middle', out_sha...  314 us
    pallas_call x1, Pallas kernels, first(): pl.pallas_call(functools.partial(first_kernel, geo), name='first', out_sh...  140 us
    dot_general x3, matrix products, local_purify(): jnp.dot(strip, full, precision=HIGHEST, preferred_element_type=jnp.float32)  136 us
    pallas_call x1, Pallas kernels, last(): pl.pallas_call(functools.partial(last_kernel, geo), name='last', out_shap...  133 us
  transfers between devices with their start and end apart: 1, of which 1 were waited for; matrix products, arithmetic and copies ran while one was open for 1% of the time, Pallas kernels for 0%

profile of v2, /device:TPU:97, one launch (start us, length us, event | category | flops | bytes accessed | tf_op | source)
XLA Modules:
  0.0 789.7 jit_solution(9038591485712625753)
XLA Ops:
  7.2 0.1 all-gather.3.cloned.1.call-start
  7.3 3.9 constant_dynamic-slice_fusion
  11.2 0.1 all-gather.3.cloned.1.call-update
  11.2 0.2 iota_compare_fusion
  11.5 0.0 copy-start.1
  11.5 0.0 copy-start.2
  11.5 3.9 select_reduce_fusion
  15.4 13.8 %psum.7 = f32[2]{0:T(128)S(1)} all-reduce(f32[2]{0:T(128)S(1)} %broadcast_select_fusion), channel_id=1, replica_groups=mesh['spin'=1,'depth'=4,'row'=4,'col'=2] {'row','col'}, use_global_device_ids=true, to_apply=%region_1.2 | all-reduce | flops 2 | bytes 16 | tf_op jit(solution)/shard_map/psum | solution.py:552
  29.2 0.0 copy-done.1
  29.2 0.2 slice_reduce_fusion.2
  29.4 0.0 copy-done.2
  29.4 0.6 dynamic_slice.20
  30.0 0.6 dynamic_slice.21
  30.6 2.7 all-gather.3.cloned.1.call-done
  33.3 6.5 multiply_subtract_fusion
  39.8 0.0 copy-start
  39.8 140.5 %first.1.full_in = f32[3584,3584]{1,0:T(8,128)} custom-call(f32[224,3584]{1,0:T(8,128)} %get-tuple-element.25.strip), custom_call_target="tpu_custom_call" | custom-call | tf_op jit(solution)/shard_map/first/pallas_call | solution.py:512
  180.3 0.0 copy-done
  180.3 44.5 %select_reduce_fusion.3 = (f32[]{:T(128)}, f32[]{:T(128)}, f32[]{:T(128)}, f32[224,3584]{1,0:T(8,128)}) fusion(f32[224,3584]{1,0:T(8,128)S(1)} %copy-done, s32[224]{0:T(256)S(1)} %iota_add_fusion, f32[3584,3584]{1,0:T(8,128)} %first.1.full_in), kind=kOutput, calls=%fused_computation.10 | convolution fusion | flops 34533130240 | bytes 57803660 | tf_op jit(solution)/shard_map/dot_general | solution.py:571
  224.8 1.9 select_maximum_fusion.4
  226.6 0.7 broadcast_in_dim.48.sums
  227.3 156.7 %middle.2 = (f32[3584,3584]{1,0:T(8,128)}, f32[224,3584]{1,0:T(8,128)}) custom-call(f32[3584,3584]{1,0:T(8,128)} %first.1.full_in, f32[224,3584]{1,0:T(8,128)} %get-tuple-element.29.sq, f32[224,3584]{1,0:T(8,128)} %get-tuple-element.25.strip, f32[8,128]{1,0:T(8,128)} %broadcast_in_dim.48.sums), custom_call_target="tpu_custom_call" | custom-call | tf_op jit(solution)/shard_map/middle/pallas_call | solution.py:519
  384.0 45.6 %select_reduce_fusion.2 = (f32[]{:T(128)}, f32[]{:T(128)}, f32[]{:T(128)}, f32[224,3584]{1,0:T(8,128)}) fusion(f32[224,3584]{1,0:T(8,128)} %get-tuple-element.9.strip, s32[224]{0:T(256)S(1)} %iota_add_fusion, f32[3584,3584]{1,0:T(8,128)} %get-tuple-element.8.full_in), kind=kOutput, calls=%fused_computation.7 | convolution fusion | flops 34533130240 | bytes 57803660 | tf_op jit(solution)/shard_map/dot_general | solution.py:571
  429.6 2.0 select_maximum_fusion.2
  431.6 0.7 broadcast_in_dim.49.sums
  432.3 157.0 %middle.3 = (f32[3584,3584]{1,0:T(8,128)}, f32[224,3584]{1,0:T(8,128)}) custom-call(f32[3584,3584]{1,0:T(8,128)} %get-tuple-element.8.full_in, f32[224,3584]{1,0:T(8,128)} %get-tuple-element.30.sq, f32[224,3584]{1,0:T(8,128)} %get-tuple-element.9.strip, f32[8,128]{1,0:T(8,128)} %broadcast_in_dim.49.sums), custom_call_target="tpu_custom_call" | custom-call | tf_op jit(solution)/shard_map/middle/pallas_call | solution.py:519
  589.3 45.6 %select_reduce_fusion.1 = (f32[]{:T(128)}, f32[]{:T(128)}, f32[]{:T(128)}, f32[224,3584]{1,0:T(8,128)}) fusion(f32[224,3584]{1,0:T(8,128)} %get-tuple-element.11.strip, s32[224]{0:T(256)S(1)} %iota_add_fusion, f32[3584,3584]{1,0:T(8,128)} %get-tuple-element.10.full_in), kind=kOutput, calls=%fused_computation.4 | convolution fusion | flops 34533130240 | bytes 57803660 | tf_op jit(solution)/shard_map/dot_general | solution.py:571
  634.8 1.9 select_maximum_fusion
  636.7 0.7 broadcast_in_dim.50.sums
  637.4 133.4 %last.1 = (f32[2,896,1792]{2,1,0:T(8,128)}, f32[8,128]{1,0:T(8,128)}) custom-call(f32[3584,3584]{1,0:T(8,128)} %get-tuple-element.10.full_in, f32[224,3584]{1,0:T(8,128)} %get-tuple-element.31.sq, f32[224,3584]{1,0:T(8,128)} %get-tuple-element.11.strip, f32[8,128]{1,0:T(8,128)} %broadcast_in_dim.50.sums, f32[224,3584]{1,0:T(8,128)} %get-tuple-element.26.ham), custom_call_target="tpu_custom_call" | custom-call | tf_op jit(solution)/shard_map/last/pallas_call | solution.py:529
  770.7 1.3 slice_reduce_fusion
  772.0 10.3 %copy.6 = f32[2,896,1792]{2,1,0:T(8,128)} copy(f32[2,896,1792]{2,1,0:T(8,128)} %get-tuple-element.34) | data formatting | bytes 25690112
  (4 shorter events, 0.0 us)
Async XLA Ops:
  7.2 26.1 %all-gather.3.cloned.1.call-start = ((), (), s32[]{:S(2)}) async-start(), calls=%async_computation | async-start | bytes 9633792 | tf_op jit(solution)/shard_map/all_gather | solution.py:565
  11.5 17.7 %copy-start.1 = (f32[2,2]{1,0:T(2,128)S(1)}, f32[2,2]{1,0:T(2,128)}, u32[]{:S(2)}) copy-start(f32[2,2]{1,0:T(2,128)} %param.4) | copy-start | bytes 52
  11.5 17.9 %copy-start.2 = (s32[2]{0:T(128)S(1)}, s32[2]{0:T(128)}, u32[]{:S(2)}) copy-start(s32[2]{0:T(128)} %param.5) | copy-start | bytes 28
  39.8 140.5 %copy-start = (f32[224,3584]{1,0:T(8,128)S(1)}, f32[224,3584]{1,0:T(8,128)}, u32[]{:S(2)}) copy-start(f32[224,3584]{1,0:T(8,128)} %get-tuple-element.25.strip) | copy-start | bytes 9633796
Sparse Core Ops, SparseCore 0:
  11.3 21.8 all-gather.2

commit v3 on v2

--- a/solution.py
+++ b/solution.py
@@ -176,42 +176,78 @@
     pl.semaphore_wait(barrier, len(devs))
 
 
-def transpose_region(full, row0, col0, h, w, tin, tout, sem):
-    rows, cols = pl.ds(pl.multiple_of(row0, LANE), h), pl.ds(pl.multiple_of(col0, LANE), w)
-    cp = pltpu.make_async_copy(full.at[rows, cols], tin.at[pl.ds(0, h), pl.ds(0, w)], sem)
-    cp.start()
-    cp.wait()
-
-    def body(t, carry):
-        at = pl.ds(pl.multiple_of(t * LANE, LANE), LANE)
-        tout[pl.ds(0, w), at] = tin[at, pl.ds(0, w)].T
-        return carry
-
-    lax.fori_loop(0, h // LANE, body, 0)
-    out = full.at[pl.ds(pl.multiple_of(col0, LANE), w), pl.ds(pl.multiple_of(row0, LANE), h)]
-    cp = pltpu.make_async_copy(tout.at[pl.ds(0, w), pl.ds(0, h)], out, sem)
-    cp.start()
-    cp.wait()
-
-
-def mirror_next(geo, full, k, tin, tout, sem):
-    k = rem(k, 4)
-    transpose_region(full, k * geo.blk, rem(k + 1, 4) * geo.blk, geo.blk, geo.blk, tin, tout, sem)
-
-
-def mirror_far(geo, full, k, tin, tout, sem):
-    def body(j, carry):
-        i, t = rem(k + 2 * (j // 2), 4), rem(j, 2)
-        row0 = i * geo.blk + t * geo.wide
-        col0 = rem(i + 2, 4) * geo.blk + geo.lo * rem(i // 2 + t, 2)
-        transpose_region(full, row0, col0, geo.lo, geo.wide, tin, tout, sem)
-        return carry
-
-    lax.fori_loop(0, 4, body, 0)
-
-
-def complete(geo, links, core, keeps, tin, tout, sem, done):
-    full, r = links.full, links.r
+class Mirror:
+    def __init__(self, geo, full, tin, tout, fin, fout, sem):
+        self.geo, self.full, self.tin, self.tout, self.fin, self.fout, self.sem = geo, full, tin, tout, fin, fout, sem
+
+    def next(self, k):
+        geo, blk = self.geo, self.geo.blk
+        row0, col0 = rem(k, 4) * blk, rem(k + 1, 4) * blk
+        slabs = blk // LANE
+
+        def load(t):
+            rows = pl.ds(pl.multiple_of(row0 + t * LANE, LANE), LANE)
+            return pltpu.make_async_copy(
+                self.full.at[rows, pl.ds(pl.multiple_of(col0, LANE), blk)],
+                self.tin.at[pl.ds(pl.multiple_of(t * LANE, LANE), LANE)], self.sem.at[0, t])
+
+        def store(t):
+            cols = pl.ds(pl.multiple_of(row0 + t * LANE, LANE), LANE)
+            return pltpu.make_async_copy(
+                self.tout.at[:, pl.ds(pl.multiple_of(t * LANE, LANE), LANE)],
+                self.full.at[pl.ds(pl.multiple_of(col0, LANE), blk), cols], self.sem.at[1, t])
+
+        def turn(t):
+            load(t).wait()
+            at = pl.ds(pl.multiple_of(t * LANE, LANE), LANE)
+            self.tout[:, at] = self.tin[at, :].T
+            store(t).start()
+
+        self.each(slabs, lambda t: load(t).start())
+        self.each(slabs, turn)
+        self.each(slabs, lambda t: store(t).wait())
+
+    def far(self, k):
+        geo = self.geo
+
+        def place(j):
+            i, t = rem(k + 2 * (j // 2), 4), rem(j, 2)
+            row0 = i * geo.blk + t * geo.wide
+            col0 = rem(i + 2, 4) * geo.blk + geo.lo * rem(i // 2 + t, 2)
+            return pl.multiple_of(row0, LANE), pl.multiple_of(col0, LANE)
+
+        def load(j):
+            row0, col0 = place(j)
+            return pltpu.make_async_copy(
+                self.full.at[pl.ds(row0, geo.lo), pl.ds(col0, geo.wide)], self.fin.at[j], self.sem.at[0, j])
+
+        def store(j):
+            row0, col0 = place(j)
+            return pltpu.make_async_copy(
+                self.fout.at[j], self.full.at[pl.ds(col0, geo.wide), pl.ds(row0, geo.lo)], self.sem.at[1, j])
+
+        def turn(j):
+            load(j).wait()
+            for t in range(geo.lo // LANE):
+                at = slice(t * LANE, (t + 1) * LANE)
+                self.fout[j, :, at] = self.fin[j, at, :].T
+            store(j).start()
+
+        self.each(4, lambda j: load(j).start())
+        self.each(4, turn)
+        self.each(4, lambda j: store(j).wait())
+
+    @staticmethod
+    def each(count, fn):
+        def body(t, carry):
+            fn(t)
+            return carry
+
+        lax.fori_loop(0, count, body, 0)
+
+
+def complete(links, core, keeps, mirror, done):
+    r = links.r
     near = (MATE,) if core == 0 else (below(0), above(0))
     for part in range(done, 3):
         for slot in near:
@@ -230,30 +266,39 @@
     for cp in keeps:
         cp.wait()
 
-    def sibs(slots):
+    def sibs(slots, parts=range(3)):
         for slot in slots:
-            for part in range(3):
+            for part in parts:
                 links.sib_arrive(slot, part, core)
 
+    def far_relays(lam, parts):
+        for part in parts:
+            for h in (0, 1):
+                links.relay(far(lam, h), part, core)
+
+    near = (below(0), below(1), above(0), above(1))
+    fars = [far(lam, h) for lam in (0, 1) for h in (0, 1)]
     sibs((OWN, MATE))
-    mirror_next(geo, full, r, tin, tout, sem)
+    mirror.next(r)
     if core == 1:
         for part in range(3):
             links.relay(below(1), part, core)
             links.relay(above(1), part, core)
-    sibs((below(0), below(1), above(0), above(1)))
-    mirror_next(geo, full, r + 3, tin, tout, sem)
-    mirror_next(geo, full, r + 1, tin, tout, sem)
-    links.drain((below(0), below(1), above(0), above(1)), (2,), core)
-    mirror_far(geo, full, r + 1, tin, tout, sem)
-    for part in range(3):
-        for lam in (0, 1) if core == 0 else (1,):
-            for h in (0, 1):
-                links.relay(far(lam, h), part, core)
-    sibs([far(lam, h) for lam in (0, 1) for h in (0, 1)])
-    mirror_next(geo, full, r + 2, tin, tout, sem)
-    links.drain([slot for slot in links.slots if slot[1] in (0, 2)], (2,), core)
-    mirror_far(geo, full, r, tin, tout, sem)
+    sibs(near)
+    mirror.next(r + 3)
+    if core == 0:
+        far_relays(0, range(3))
+    far_relays(1, (0,))
+    mirror.next(r + 1)
+    far_relays(1, (1,))
+    links.drain(near, (2,), core)
+    mirror.far(r + 1)
+    far_relays(1, (2,))
+    sibs(fars, (0, 1))
+    mirror.next(r + 2)
+    sibs(fars, (2,))
+    links.drain((OWN, MATE, *fars), (2,), core)
+    mirror.far(r)
     links.drain(list(links.slots), range(3), core)
 
 
@@ -264,17 +309,39 @@
     return pltpu.make_async_copy(own.at[:, cols], links.full.at[pl.ds(pl.multiple_of(row0, 8), geo.strip), cols], sem.at[part])
 
 
-def first_kernel(geo, strip, full, send_sem, recv_sem, sib_send, sib_recv, keep_sem, tin, tout, tsem):
+def first_kernel(geo, ham, part_trace, bounds, strip, full, send_sem, recv_sem, sib_send, sib_recv, keep_sem, tin, tout, fin,
+                 fout, tsem, mid, tot, box, red_send, red_recv):
     links = Links(geo, strip, full, send_sem, recv_sem, sib_send, sib_recv)
-    enter([links.up, links.down, links.mate, links.sibling])
+    red = Reduce(geo, part_trace, mid, box, red_send, red_recv)
+    enter(red.round1 + red.round2)
+    red.start(True)
+    mid[...] = red.total(True)
+    strip[...] = -ham[...]
+    red.start(False)
+    tot[...] = red.total(False)
+    n = geo.order
+    mu = tot[0:1, 0:1] / n
+    occ, low, high = (bounds[j:j + 1, 0:1] for j in range(3))
+    lam = jnp.minimum(occ / (high - mu), (n - occ) / (mu - low))
+    add, scale = (lam * mu + occ) / n, lam / n
+    row0 = links.r * geo.blk + (links.e * 2 + links.c) * geo.strip
+
+    def shift(t, carry):
+        cols = pl.ds(pl.multiple_of(t * LANE, LANE), LANE)
+        shape = (geo.strip, LANE)
+        diag = (lax.broadcasted_iota(jnp.int32, shape, 0) + row0) == (lax.broadcasted_iota(jnp.int32, shape, 1) + t * LANE)
+        strip[:, cols] = jnp.where(diag, add, 0.0) + scale * strip[:, cols]
+        return carry
+
+    lax.fori_loop(0, n // LANE, shift, 0)
     keeps = [keep_copy(links, strip, part, keep_sem) for part in range(4)]
 
     def run(core):
+        for cp in keeps:
+            cp.start()
         for part in range(3):
             links.forward(OWN, part, core)
-        for cp in keeps:
-            cp.start()
-        complete(geo, links, core, keeps, tin, tout, tsem, 0)
+        complete(links, core, keeps, Mirror(geo, full, tin, tout, fin, fout, tsem), 0)
 
     per_core(links.c, run)
 
@@ -333,9 +400,10 @@
     lax.fori_loop(0, 4 * per, body, 0)
 
 
-def mid_kernel(geo, full_in, sq, strip, sums, full, new, send_sem, recv_sem, sib_send, sib_recv, keep_sem, tin, tout, tsem,
-               buf, acc, buf_sem, mid, tot, box, red_send, red_recv):
+def mid_kernel(geo, full_in, sq, strip, sums, full, new, send_sem, recv_sem, sib_send, sib_recv, keep_sem, tin, tout, fin, fout,
+               tsem, buf, acc, buf_sem, mid, tot, box, red_send, red_recv):
     links = Links(geo, new, full, send_sem, recv_sem, sib_send, sib_recv)
+    mirror = Mirror(geo, full, tin, tout, fin, fout, tsem)
     red = Reduce(geo, sums, mid, box, red_send, red_recv)
     red.src_total = tot
     enter(red.round1 + red.round2)
@@ -358,7 +426,7 @@
 
     cube_loop(geo, red, links.r, full_in, sq, strip, new, buf, acc, buf_sem, hook)
     keeps[3].start()
-    per_core(links.c, lambda core: complete(geo, links, core, keeps, tin, tout, tsem, 1))
+    per_core(links.c, lambda core: complete(links, core, keeps, mirror, 1))
 
 
 def last_kernel(geo, full_in, sq, strip, sums, ham, dens, energy, new, send_sem, recv_sem, sib_send, sib_recv, keep_sem,
@@ -495,7 +563,8 @@
 
 def link_scratch(geo):
     return [DMA((9, 3)), DMA((10, 3)), DMA((10, 3)), DMA((10, 3)), DMA((4,)),
-            pltpu.VMEM((geo.blk, geo.blk), jnp.float32), pltpu.VMEM((geo.blk, geo.blk), jnp.float32), DMA]
+            pltpu.VMEM((geo.blk, geo.blk), jnp.float32), pltpu.VMEM((geo.blk, geo.blk), jnp.float32),
+            pltpu.VMEM((4, geo.lo, geo.wide), jnp.float32), pltpu.VMEM((4, geo.wide, geo.lo), jnp.float32), DMA((2, max(4, geo.blk // LANE)))]
 
 
 def cube_scratch(geo):
@@ -508,11 +577,13 @@
     return pltpu.CompilerParams(collective_id=call, has_side_effects=True)
 
 
-def first(geo, strip, call):
+def first(geo, ham, part_trace, bounds, call):
     return pl.pallas_call(
         functools.partial(first_kernel, geo), name="first",
-        out_shape=jax.ShapeDtypeStruct((geo.order, geo.order), jnp.float32),
-        in_specs=[VM], out_specs=ANY, scratch_shapes=link_scratch(geo), compiler_params=params(call))(strip)
+        out_shape=(jax.ShapeDtypeStruct((geo.strip, geo.order), jnp.float32),
+                   jax.ShapeDtypeStruct((geo.order, geo.order), jnp.float32)),
+        in_specs=[VM, VM, VM], out_specs=(VM, ANY), scratch_shapes=link_scratch(geo) + cube_scratch(geo)[3:],
+        compiler_params=params(call))(ham, part_trace, bounds)
 
 
 def middle(geo, full, sq, strip, sums, call):
@@ -544,33 +615,23 @@
         r = lax.axis_index("row")
         c = lax.axis_index("col")
         m, e = d // geo.layers, d % geo.layers
-        per_col = geo.rows // geo.cols
-        on_diag = (r // per_col) == c
-        diag_start = (r % per_col) * geo.blk
-        square = lax.dynamic_slice_in_dim(ham, diag_start, geo.blk, axis=2)
-        tr = jnp.where(on_diag, jnp.trace(square, axis1=1, axis2=2), 0.0)
-        mu = lax.psum(tr, ("row", "col")) / n
-        occ = occ_count.astype(jnp.float32)
-        lam = jnp.minimum(occ / (spec_bounds[:, 1] - mu), (n - occ) / (mu - spec_bounds[:, 0]))
-        add = (lam * mu + occ) / n
-        scale = lam / n
-
         row0 = r * geo.blk + (e * 2 + c) * geo.strip
         rows = lax.broadcasted_iota(jnp.int32, (geo.strip, n), 0) + row0
         cols = lax.broadcasted_iota(jnp.int32, (geo.strip, n), 1)
         diag = rows == cols
 
         ham_m = lax.dynamic_index_in_dim(ham, m, axis=0, keepdims=False)
-        layer_rows = lax.dynamic_slice_in_dim(ham_m, e * 2 * geo.strip, 2 * geo.strip, axis=0)
-        layer_all = lax.all_gather(layer_rows, "col", axis=1, tiled=True)
-        ham_strip = lax.dynamic_slice_in_dim(layer_all, c * geo.strip, geo.strip, axis=0)
-        strip = jnp.where(diag, add[m], 0.0) - scale[m] * ham_strip
-
-        full = first(geo, strip, 0)
+        own = lax.dynamic_slice_in_dim(ham_m, (e * 2 + c) * geo.strip, geo.strip, axis=0)
+        theirs = lax.dynamic_slice_in_dim(ham_m, (e * 2 + 1 - c) * geo.strip, geo.strip, axis=0)
+        got = lax.ppermute(theirs, "col", [(0, 1), (1, 0)])
+        ham_strip = jnp.concatenate([jnp.where(c == 0, own, got), jnp.where(c == 0, got, own)], axis=1)
+        tile = lambda rows: jnp.broadcast_to(jnp.pad(jnp.stack(rows), (0, 8 - len(rows)))[:, None], TILE)
+        trace = tile([jnp.sum(jnp.where(diag, ham_strip, 0.0))])
+        bounds = tile([occ_count[m].astype(jnp.float32), spec_bounds[m, 0], spec_bounds[m, 1]])
+        strip, full = first(geo, ham_strip, trace, bounds, 0)
         for step in range(STEPS):
             sq = jnp.dot(strip, full, precision=HIGHEST, preferred_element_type=jnp.float32)
-            sums = jnp.stack([jnp.sum(jnp.where(diag, strip, 0.0)), jnp.sum(strip * strip), jnp.sum(sq * strip)])
-            sums = jnp.broadcast_to(jnp.pad(sums, (0, 5))[:, None], TILE)
+            sums = tile([jnp.sum(jnp.where(diag, strip, 0.0)), jnp.sum(strip * strip), jnp.sum(sq * strip)])
             if step < STEPS - 1:
                 full, strip = middle(geo, full, sq, strip, sums, step + 1)
         density, pair = last(geo, full, sq, strip, sums, ham_strip, STEPS)

time: 797 us -> 730 us (0.916)
  Pallas kernels: 587 us -> 553 us
  blocking collectives: 13.8 us -> 0 us
  between operations: 14.6 us -> 1.55 us
    pallas_call x2, Pallas kernels: 314 us -> 284 us  [middle(): pl.pallas_call(functools.partial(mid_kernel, geo), name='middle', out_sha...]
    psum x1 -> x0, blocking collectives: 13.8 us -> none  [local_purify(): mu = lax.psum(tr, ('row', 'col')) / n]
  transfers between devices with their start and end apart: 1 -> 1, of which waited for: 1 -> 0; matrix products, arithmetic and copies ran while one was open for 1% -> 0% of each run, Pallas kernels for 0% -> 0%
where the time goes in v3:
time: 730 us; the launch traced here: 724 us
  Pallas kernels  553 us (76%)
  matrix products  137 us (19%)
  local copies, waits for them, and re-layouts  18.4 us (3%)
  other arithmetic  11.6 us (2%)
    pallas_call x2, Pallas kernels, middle(): pl.pallas_call(functools.partial(mid_kernel, geo), name='middle', out_sha...  284 us
    dot_general x3, matrix products, local_purify(): jnp.dot(strip, full, precision=HIGHEST, preferred_element_type=jnp.float32)  137 us
    pallas_call x1, Pallas kernels, first(): pl.pallas_call(functools.partial(first_kernel, geo), name='first', out_sh...  135 us
    pallas_call x1, Pallas kernels, last(): pl.pallas_call(functools.partial(last_kernel, geo), name='last', out_shap...  134 us
  transfers between devices with their start and end apart: 1, of which 0 were waited for; matrix products, arithmetic and copies ran while one was open for 0% of the time, Pallas kernels for 0%

profile of v3, /device:TPU:97, one launch (start us, length us, event | category | flops | bytes accessed | tf_op | source)
XLA Modules:
  0.0 723.8 jit_solution(1010511414617750834)
XLA Ops:
  0.6 0.0 copy-start.1
  0.6 0.0 copy-start
  0.7 1.6 dynamic-slice_bitcast_fusion
  2.3 2.1 collective-permute-start
  4.4 0.0 copy-done.1
  4.4 0.6 dynamic_slice.25
  5.6 0.0 copy-done
  5.6 0.6 constant_dynamic-slice_fusion
  6.2 1.4 select_maximum_fusion.6
  7.6 0.0 collective-permute-done
  7.6 1.7 bitcast_select_fusion.1
  9.3 2.5 select_reduce_fusion.3
  11.9 0.6 pad.17
  12.5 0.7 broadcast_in_dim.19.bounds
  13.2 0.7 broadcast_in_dim.18.part_trace
  13.8 135.0 %first.1 = (f32[224,3584]{1,0:T(8,128)}, f32[3584,3584]{1,0:T(8,128)}) custom-call(f32[224,3584]{1,0:T(8,128)} %get-tuple-element.30.ham, f32[8,128]{1,0:T(8,128)} %broadcast_in_dim.18.part_trace, f32[8,128]{1,0:T(8,128)} %broadcast_in_dim.19.bounds), custom_call_target="tpu_custom_call" | custom-call | tf_op jit(solution)/shard_map/first/pallas_call | solution.py:581
  148.8 45.6 %select_reduce_fusion.2 = (f32[]{:T(128)}, f32[]{:T(128)}, f32[]{:T(128)}, f32[224,3584]{1,0:T(8,128)}) fusion(f32[224,3584]{1,0:T(8,128)} %get-tuple-element.11.strip, s32[224]{0:T(256)S(1)} %iota_add_fusion, f32[3584,3584]{1,0:T(8,128)} %get-tuple-element.10.full_in), kind=kOutput, calls=%fused_computation.9 | convolution fusion | flops 34533130240 | bytes 57803660 | tf_op jit(solution)/shard_map/dot_general | solution.py:633
  194.5 2.0 select_maximum_fusion.4
  196.5 0.7 broadcast_in_dim.20.sums
  197.2 141.8 %middle.2 = (f32[3584,3584]{1,0:T(8,128)}, f32[224,3584]{1,0:T(8,128)}) custom-call(f32[3584,3584]{1,0:T(8,128)} %get-tuple-element.10.full_in, f32[224,3584]{1,0:T(8,128)} %get-tuple-element.33.sq, f32[224,3584]{1,0:T(8,128)} %get-tuple-element.11.strip, f32[8,128]{1,0:T(8,128)} %broadcast_in_dim.20.sums), custom_call_target="tpu_custom_call" | custom-call | tf_op jit(solution)/shard_map/middle/pallas_call | solution.py:590
  339.0 45.7 %select_reduce_fusion.1 = (f32[]{:T(128)}, f32[]{:T(128)}, f32[]{:T(128)}, f32[224,3584]{1,0:T(8,128)}) fusion(f32[224,3584]{1,0:T(8,128)} %get-tuple-element.13.strip, s32[224]{0:T(256)S(1)} %iota_add_fusion, f32[3584,3584]{1,0:T(8,128)} %get-tuple-element.12.full_in), kind=kOutput, calls=%fused_computation.6 | convolution fusion | flops 34533130240 | bytes 57803660 | tf_op jit(solution)/shard_map/dot_general | solution.py:633
  384.6 2.0 select_maximum_fusion.2
  386.7 0.7 broadcast_in_dim.21.sums
  387.3 141.9 %middle.3 = (f32[3584,3584]{1,0:T(8,128)}, f32[224,3584]{1,0:T(8,128)}) custom-call(f32[3584,3584]{1,0:T(8,128)} %get-tuple-element.12.full_in, f32[224,3584]{1,0:T(8,128)} %get-tuple-element.34.sq, f32[224,3584]{1,0:T(8,128)} %get-tuple-element.13.strip, f32[8,128]{1,0:T(8,128)} %broadcast_in_dim.21.sums), custom_call_target="tpu_custom_call" | custom-call | tf_op jit(solution)/shard_map/middle/pallas_call | solution.py:590
  529.2 45.7 %select_reduce_fusion = (f32[]{:T(128)}, f32[]{:T(128)}, f32[]{:T(128)}, f32[224,3584]{1,0:T(8,128)}) fusion(f32[224,3584]{1,0:T(8,128)} %get-tuple-element.15.strip, s32[224]{0:T(256)S(1)} %iota_add_fusion, f32[3584,3584]{1,0:T(8,128)} %get-tuple-element.14.full_in), kind=kOutput, calls=%fused_computation.3 | convolution fusion | flops 34533130240 | bytes 57803660 | tf_op jit(solution)/shard_map/dot_general | solution.py:633
  574.9 2.0 select_maximum_fusion
  576.9 0.7 broadcast_in_dim.42.sums
  577.5 134.4 %last.1 = (f32[2,896,1792]{2,1,0:T(8,128)}, f32[8,128]{1,0:T(8,128)}) custom-call(f32[3584,3584]{1,0:T(8,128)} %get-tuple-element.14.full_in, f32[224,3584]{1,0:T(8,128)} %get-tuple-element.35.sq, f32[224,3584]{1,0:T(8,128)} %get-tuple-element.15.strip, f32[8,128]{1,0:T(8,128)} %broadcast_in_dim.42.sums, f32[224,3584]{1,0:T(8,128)} %get-tuple-element.30.ham), custom_call_target="tpu_custom_call" | custom-call | tf_op jit(solution)/shard_map/last/pallas_call | solution.py:600
  712.0 1.3 slice_reduce_fusion
  713.3 10.3 %copy.6 = f32[2,896,1792]{2,1,0:T(8,128)} copy(f32[2,896,1792]{2,1,0:T(8,128)} %get-tuple-element.38) | data formatting | bytes 25690112
  (1 shorter events, 0.0 us)
Async XLA Ops:
  0.6 3.8 copy-start.1
  0.6 5.0 copy-start
  2.3 5.3 collective-permute-start
